TPU v7x, 32 devices: a whole 2x2x4 slice. The times are simulated.
32 devices in a mesh: tm: 8 (over y, x, core), series: 4 (over z).
Axes of the slice: x: 2, y: 2, z: 4, core: 2. Of those that a mesh axis runs over, the one named last changes fastest.
Arguments:
- tokens: bfloat16 [8, 4096, 1024], P('series', 'tm'), may hold values from -6 to 6
- gate_proj: bfloat16 [1024, 2048], replicated, may hold values from -0.1875 to 0.1875
- input_proj: bfloat16 [1024, 2304], replicated, may hold values from -0.1875 to 0.1875
- step_proj: bfloat16 [1024, 32], replicated, may hold values from -0.1875 to 0.1875
- conv_kernel: float32 [4, 2304], replicated, may hold values from -3 to 3
- conv_bias: float32 [2304], replicated, may hold values from -0.5 to 0.5
- step_bias: float32 [32], replicated, may hold values from -1 to 1
- decay_rate: float32 [32], replicated, may hold values from 0.00012207031 to 0.1
- skip_gain: float32 [32], replicated, may hold values from 0.5 to 1.5
- norm_gain: float32 [2048], replicated, may hold values from 0.1 to 1.9
- out_proj: bfloat16 [2048, 1024], replicated, may hold values from -0.125 to 0.125
- lengths: int32 [8], P('series'), may hold values from 256 to 4096, as said below
- slot_series: int32 [8], P('series'), may hold values from 0 to 7, each once
Outputs:
- mixed: bfloat16 [8, 4096, 1024], P('series', 'tm')
Inputs may be any that keep to these rules, and one draw needn't show every extreme that they name: `lengths`: multiples of 256; some series has the full 4096. `slot_series`: each series number appears once.
All inputs are finite; a program needn't handle non-finite values.
Results may differ from a plain program's by a relative error of at most 0.0054.
Values may be sent and summed in bfloat16 or wider, within the bound.
A program may use at most 128 MiB of HBM per device.

v0:
```python
import jax
import jax.numpy as jnp
from jax import lax
from jax.sharding import PartitionSpec as P

DI = 2048
H = 32
P_SIZE = 64
N = 128
BLOCK = 256


epsilon = 1e-05


def shifted(shard, axis, by):
    count = lax.axis_size(axis)
    pairs = [(i, i + by) for i in range(count) if 0 <= i + by < count]
    return lax.ppermute(shard, axis, pairs)


def carried_in(value, axis, join, neutral):
    count, mine = (lax.axis_size(axis), lax.axis_index(axis))
    pieces = jax.tree.map(lambda part: lax.all_gather(part, axis), value)
    total = jax.tree.map(
        lambda part, zero: jnp.full_like(part, 0) + jnp.asarray(zero, part.dtype), value, neutral
    )

    def step(position, total):
        longer = join(total, jax.tree.map(lambda part: part[position], pieces))
        return jax.tree.map(lambda new, old: jnp.where(position < mine, new, old), longer, total)

    return lax.fori_loop(0, count - 1, step, total)


def block_terms(inputs_x, inputs_b, inputs_c, step_sizes, decay_rate, skip_gain):
    width_q = inputs_x.shape[0]
    cumulative = jnp.cumsum(-step_sizes * decay_rate[None, :], axis=0)
    heads_cum = cumulative.T
    causal = jnp.tril(jnp.ones((width_q, width_q), dtype=bool))[None]
    segment = heads_cum[:, :, None] - heads_cum[:, None, :]
    decays = jnp.where(causal, jnp.exp(jnp.where(causal, segment, 0.0)), 0.0)
    scores = jnp.dot(inputs_c, inputs_b.T, preferred_element_type=jnp.float32)
    weights = (decays * scores[None] * step_sizes.T[:, None, :]).astype(jnp.bfloat16)
    intra = jnp.einsum("hts,shp->thp", weights, inputs_x, preferred_element_type=jnp.float32)
    partial_out = intra + skip_gain[None, :, None] * inputs_x.astype(jnp.float32)
    end_weight = jnp.exp(cumulative[-1][None, :] - cumulative) * step_sizes
    weighted_x = (inputs_x.astype(jnp.float32) * end_weight[:, :, None]).astype(jnp.bfloat16)
    increment = jnp.einsum("shp,sn->hpn", weighted_x, inputs_b, preferred_element_type=jnp.float32)
    return (partial_out, cumulative, increment)


def body(
    tokens,
    gate_proj,
    input_proj,
    step_proj,
    conv_kernel,
    conv_bias,
    step_bias,
    decay_rate,
    skip_gain,
    norm_gain,
    out_proj,
    lengths,
    slot_series,
):
    series_here, local_steps, model_width = tokens.shape
    flat_tokens = tokens.reshape(series_here * local_steps, model_width)
    gate = jnp.dot(flat_tokens, gate_proj, preferred_element_type=jnp.float32)
    mixed_raw = jnp.dot(flat_tokens, input_proj, preferred_element_type=jnp.float32).astype(
        jnp.bfloat16
    )
    mixed_raw = mixed_raw.reshape(series_here, local_steps, DI + 2 * N)
    step_raw = jnp.dot(flat_tokens, step_proj, preferred_element_type=jnp.float32).reshape(
        series_here, local_steps, H
    )
    kernel_len = conv_kernel.shape[0]
    rim_steps = mixed_raw[:, local_steps - (kernel_len - 1) :, :]
    earlier_rim = shifted(rim_steps, "tm", 1)
    padded = jnp.concatenate([earlier_rim, mixed_raw], axis=1)
    convolved = jnp.zeros(mixed_raw.shape, jnp.float32) + conv_bias[None, None, :]
    for offset in range(kernel_len):
        convolved = convolved + conv_kernel[offset][None, None, :] * padded[
            :, offset : offset + local_steps
        ].astype(jnp.float32)
    activated = jax.nn.silu(convolved)
    all_lengths = lax.all_gather(lengths, "series", axis=0, tiled=True)
    matches = slot_series[:, None] == jnp.arange(all_lengths.shape[0], dtype=jnp.int32)[None, :]
    my_lengths = jnp.sum(jnp.where(matches, all_lengths[None, :], 0), axis=1)
    time_offset = lax.axis_index("tm") * local_steps
    positions = time_offset + jnp.arange(local_steps, dtype=jnp.int32)
    live = (positions[None, :] < my_lengths[:, None]).astype(jnp.float32)
    block_count = local_steps // BLOCK
    inputs_x = (
        activated[:, :, :DI]
        .astype(jnp.bfloat16)
        .reshape(series_here, block_count, BLOCK, H, P_SIZE)
    )
    inputs_b = (
        activated[:, :, DI : DI + N]
        .astype(jnp.bfloat16)
        .reshape(series_here, block_count, BLOCK, N)
    )
    inputs_c = (
        activated[:, :, DI + N :].astype(jnp.bfloat16).reshape(series_here, block_count, BLOCK, N)
    )
    step_sizes = (jax.nn.softplus(step_raw + step_bias[None, None, :]) * live[:, :, None]).reshape(
        series_here, block_count, BLOCK, H
    )
    block_starts = time_offset + jnp.arange(block_count, dtype=jnp.int32) * BLOCK
    block_live = block_starts[None, :] < my_lengths[:, None]

    def compute_terms(block_x, block_b, block_c, block_dt):
        return block_terms(block_x, block_b, block_c, block_dt, decay_rate, skip_gain)

    def series_pass(pieces):
        series_x, series_b, series_c, series_dt, series_live = pieces

        def advance(carried, block_pieces):
            block_x, block_b, block_c, block_dt, block_flag = block_pieces
            partial_out, cumulative, increment = compute_terms(block_x, block_b, block_c, block_dt)
            new_state = jnp.exp(cumulative[-1])[:, None, None] * carried + increment
            return (new_state, (partial_out, cumulative, carried))

        start_state = jnp.zeros((H, P_SIZE, N), jnp.float32)
        return lax.scan(
            advance, start_state, (series_x, series_b, series_c, series_dt, series_live)
        )

    end_states, (partials, cumulatives, befores) = lax.map(
        series_pass, (inputs_x, inputs_b, inputs_c, step_sizes, block_live)
    )
    block_decay = cumulatives[:, :, -1, :]
    device_decay = jnp.sum(block_decay, axis=1)

    def combine(before_part, after_part):
        return (
            before_part[0] + after_part[0],
            jnp.exp(after_part[0])[:, :, None, None] * before_part[1] + after_part[1],
        )

    prefix_parts = carried_in(
        (device_decay, end_states),
        "tm",
        combine,
        (jnp.zeros_like(device_decay), jnp.zeros_like(end_states)),
    )
    incoming = prefix_parts[1]
    before_decay = jnp.cumsum(block_decay, axis=1) - block_decay
    states_in = jnp.exp(before_decay)[:, :, :, None, None] * incoming[:, None] + befores
    states_bf = states_in.astype(jnp.bfloat16)
    inter = jnp.einsum("sctn,schpn->scthp", inputs_c, states_bf, preferred_element_type=jnp.float32)
    outputs = partials + jnp.exp(cumulatives)[:, :, :, :, None] * inter
    outputs = outputs.reshape(series_here * local_steps, DI)
    gated = outputs * jax.nn.silu(gate)
    scale = lax.rsqrt(jnp.mean(gated * gated, axis=1, keepdims=True) + epsilon)
    normed = (gated * scale * norm_gain[None, :]).astype(jnp.bfloat16)
    result = jnp.dot(normed, out_proj, preferred_element_type=jnp.float32).reshape(
        series_here, local_steps, model_width
    )
    return (result * live[:, :, None]).astype(jnp.bfloat16)


def solution(mesh):
    in_specs = (
        P("series", "tm", None),
        P(),
        P(),
        P(),
        P(),
        P(),
        P(),
        P(),
        P(),
        P(),
        P(),
        P("series"),
        P("series"),
    )
    out_specs = P("series", "tm", None)
    return jax.shard_map(body, mesh=mesh, in_specs=in_specs, out_specs=out_specs, check_vma=False)
```

profile of v0, /device:TPU:0, one launch (start us, length us, event | category | flops | bytes accessed | tf_op | source)
XLA Modules:
  0.0 326.1 jit_solution(9669011082025919864)
XLA Ops:
  6.5 1.6 copy-done
  8.2 7.6 %convolution_convert_fusion = bf16[1024,2304]{1,0:T(8,128)(2,1)S(1)} fusion(bf16[1024,1024]{1,0:T(8,128)(2,1)S(1)} %bitcast.171, bf16[1024,2304]{1,0:T(8,128)(2,1)} %param.21), kind=kOutput, calls=%fused_computation.64 | convolution fusion | flops 4834197504 | bytes 11534336 | tf_op jit(solution)/shard_map/dot_general | solution.py:71
  15.8 2.2 copy-done.3
  18.0 2.4 collective-permute-start
  22.0 9.3 %all-reduce = s32[8]{0:T(128)S(1)} all-reduce(s32[8]{0:T(128)S(1)} %dynamic-update-slice), channel_id=1, replica_groups=mesh['tm'=8,'series'=4] {'series'}, use_global_device_ids=true, to_apply=%add | all-reduce | flops 8 | bytes 64
  31.5 0.8 fusion.35
  32.4 6.6 %copy.59 = bf16[2,512,2304]{1,2,0:T(8,128)(2,1)} copy(bf16[2,512,2304]{2,1,0:T(8,128)(2,1)} %bitcast.177) | data formatting | bytes 9437184 | tf_op jit(solution)/shard_map/reshape | solution.py:74
  39.1 0.7 reshape.154
  40.5 14.5 %multiply_convert_fusion.5 = bf16[2,512,2304]{1,2,0:T(8,128)(2,1)S(1)} fusion(bf16[2,512,2304]{1,2,0:T(8,128)(2,1)} %copy.59, bf16[2,3,2304]{1,2,0:T(8,128)(2,1)S(1)} %copy.58, f32[2304]{0:T(1024)S(1)} %get-tuple-element.337, f32[2304]{0:T(1024)S(1)} %get-tuple-element.338, f32[2304]{0:T(1024)S(1)} %get-tuple-element.336, f32[2304]{0:T(1024)S(1)} %get-tuple-element.335, ...), kind=kLoop, calls=%fused_computation.55 | loop fusion | flops 61341696 | bytes 9510912 | tf_op jit(solution)/shard_map/convert.2
  55.0 2.2 slice.71
  57.3 0.8 copy.62
  58.1 0.8 copy.61
  58.9 6.9 %reshape.151 = bf16[2,2,256,32,64]{2,1,4,3,0:T(2,128)(2,1)} reshape(bf16[2,512,2048]{1,2,0:T(8,128)(2,1)} %slice.71) | data formatting | bytes 8388608 | tf_op jit(solution)/shard_map/reshape | solution.py:98
  65.9 75.5 %while.48 = (s32[]{:T(128)}, f32[2,32,64,128]{3,2,1,0:T(8,128)}, f32[2,2,256,32,64]{2,4,3,1,0:T(8,128)}, f32[2,2,256,32]{2,3,1,0:T(8,128)}, f32[2,2,32,64,128]{4...) while((s32[]{:T(128)}, f32[2,32,64,128]{3,2,1,0:T(8,128)}, ...), condition=%wide.region_6.7_spmd, body=%wide.region_1.6_spmd.sunk | while | flops 437370976 | bytes 94643872 | solution.py:131
  65.9 1.0 dynamic-slice_bitcast_fusion.5
  66.9 3.3 %constant_dynamic-slice_fusion.5 = bf16[1,2,256,32,64]{2,1,4,3,0:T(2,128)(2,1)S(1)} fusion(bf16[2,2,256,32,64]{2,1,4,3,0:T(2,128)(2,1)} %get-tuple-element.684, s32[]{:T(128)} %get-tuple-element.663), kind=kLoop, calls=%fused_computation.53.clone.1 | loop fusion | bytes 4194308 | tf_op jit(solution)/shard_map/while/body/jit(dynamic_index_in_dim)/dynamic_slice | solution.py:131
  70.2 1.8 copy.94
  71.9 0.8 constant_dynamic-slice_fusion.4
  72.8 20.7 %while.50 = (s32[]{:T(128)}, f32[32,64,128]{2,1,0:T(8,128)S(1)}, f32[2,256,32,64]{1,3,2,0:T(8,128)}, f32[2,256,32]{1,2,0:T(8,128)}, f32[2,32,64,128]{3,2,1,0:T(8...) while((s32[]{:T(128)}, f32[32,64,128]{2,1,0:T(8,128)S(1)}, ...), condition=%wide.region_5.5_spmd.clone, body=%wide.region_2.4_spmd.clone.sunk | while | flops 437370976 | bytes 10887844 | solution.py:127
  74.0 5.4 %bitcast_dynamic-update-slice_fusion.18 = f32[2,256,32,64]{1,3,2,0:T(8,128)} fusion(f32[2,256,32,64]{1,3,2,0:T(8,128)} %get-tuple-element.621, s32[]{:T(128)} %get-tuple-element.619, f32[32,256]{1,0:T(8,128)S(1)} %dynamic-slice_bitcast_fusion.6, f32[256,256]{1,0:T(8,128)S(1)} %fusion.62, f32[32,256]{1,0:T(8,128)S(1)} %get-tuple-element.604, ...), kind=kOutput, calls=%fused_computation.11.clone.1 | convolution fusion | flops 282591232 | bytes 4621824 | tf_op jit(solution)/shard_map/while/body/eval_jaxpr/while/body/eval_jaxpr/hts,shp->thp/dot_general | solution.py:45
  79.7 1.1 bitcast_dynamic-update-slice_fusion.20
  80.8 1.8 convolution_add_fusion.3
  84.4 5.3 %bitcast_dynamic-update-slice_fusion.18 = f32[2,256,32,64]{1,3,2,0:T(8,128)} fusion(f32[2,256,32,64]{1,3,2,0:T(8,128)} %get-tuple-element.621, s32[]{:T(128)} %get-tuple-element.619, f32[32,256]{1,0:T(8,128)S(1)} %dynamic-slice_bitcast_fusion.6, f32[256,256]{1,0:T(8,128)S(1)} %fusion.62, f32[32,256]{1,0:T(8,128)S(1)} %get-tuple-element.604, ...), kind=kOutput, calls=%fused_computation.11.clone.1 | convolution fusion | flops 282591232 | bytes 4621824 | tf_op jit(solution)/shard_map/while/body/eval_jaxpr/while/body/eval_jaxpr/hts,shp->thp/dot_general | solution.py:45
  90.0 1.1 bitcast_dynamic-update-slice_fusion.20
  91.1 1.8 convolution_add_fusion.3
  93.5 5.0 %bitcast_dynamic-update-slice_fusion.15 = f32[2,2,256,32,64]{2,4,3,1,0:T(8,128)} fusion(f32[2,2,256,32,64]{2,4,3,1,0:T(8,128)} %get-tuple-element.665, s32[]{:T(128)} %get-tuple-element.663, f32[2,256,32,64]{1,3,2,0:T(8,128)} %get-tuple-element.583), kind=kLoop, calls=%fused_computation.45.clone.1 | loop fusion | bytes 8389120 | tf_op jit(solution)/shard_map/while/body/jit(dynamic_update_index_in_dim)/dynamic_update_slice | solution.py:131
  98.8 1.0 copy-done.6
  99.9 1.0 copy-done.5
  100.8 1.3 copy-done.7
  102.1 0.8 bitcast_dynamic-update-slice_fusion.16
  103.7 1.0 dynamic-slice_bitcast_fusion.5
  104.6 3.3 %constant_dynamic-slice_fusion.5 = bf16[1,2,256,32,64]{2,1,4,3,0:T(2,128)(2,1)S(1)} fusion(bf16[2,2,256,32,64]{2,1,4,3,0:T(2,128)(2,1)} %get-tuple-element.684, s32[]{:T(128)} %get-tuple-element.663), kind=kLoop, calls=%fused_computation.53.clone.1 | loop fusion | bytes 4194308 | tf_op jit(solution)/shard_map/while/body/jit(dynamic_index_in_dim)/dynamic_slice | solution.py:131
  107.9 1.8 copy.94
  109.7 0.8 constant_dynamic-slice_fusion.4
  110.6 20.7 %while.50 = (s32[]{:T(128)}, f32[32,64,128]{2,1,0:T(8,128)S(1)}, f32[2,256,32,64]{1,3,2,0:T(8,128)}, f32[2,256,32]{1,2,0:T(8,128)}, f32[2,32,64,128]{3,2,1,0:T(8...) while((s32[]{:T(128)}, f32[32,64,128]{2,1,0:T(8,128)S(1)}, ...), condition=%wide.region_5.5_spmd.clone, body=%wide.region_2.4_spmd.clone.sunk | while | flops 437370976 | bytes 10887844 | solution.py:127
  111.8 5.4 %bitcast_dynamic-update-slice_fusion.18 = f32[2,256,32,64]{1,3,2,0:T(8,128)} fusion(f32[2,256,32,64]{1,3,2,0:T(8,128)} %get-tuple-element.621, s32[]{:T(128)} %get-tuple-element.619, f32[32,256]{1,0:T(8,128)S(1)} %dynamic-slice_bitcast_fusion.6, f32[256,256]{1,0:T(8,128)S(1)} %fusion.62, f32[32,256]{1,0:T(8,128)S(1)} %get-tuple-element.604, ...), kind=kOutput, calls=%fused_computation.11.clone.1 | convolution fusion | flops 282591232 | bytes 4621824 | tf_op jit(solution)/shard_map/while/body/eval_jaxpr/while/body/eval_jaxpr/hts,shp->thp/dot_general | solution.py:45
  117.5 1.1 bitcast_dynamic-update-slice_fusion.20
  118.6 1.8 convolution_add_fusion.3
  122.2 5.3 %bitcast_dynamic-update-slice_fusion.18 = f32[2,256,32,64]{1,3,2,0:T(8,128)} fusion(f32[2,256,32,64]{1,3,2,0:T(8,128)} %get-tuple-element.621, s32[]{:T(128)} %get-tuple-element.619, f32[32,256]{1,0:T(8,128)S(1)} %dynamic-slice_bitcast_fusion.6, f32[256,256]{1,0:T(8,128)S(1)} %fusion.62, f32[32,256]{1,0:T(8,128)S(1)} %get-tuple-element.604, ...), kind=kOutput, calls=%fused_computation.11.clone.1 | convolution fusion | flops 282591232 | bytes 4621824 | tf_op jit(solution)/shard_map/while/body/eval_jaxpr/while/body/eval_jaxpr/hts,shp->thp/dot_general | solution.py:45
  127.8 1.1 bitcast_dynamic-update-slice_fusion.20
  128.9 1.8 convolution_add_fusion.3
  131.3 5.0 %bitcast_dynamic-update-slice_fusion.15 = f32[2,2,256,32,64]{2,4,3,1,0:T(8,128)} fusion(f32[2,2,256,32,64]{2,4,3,1,0:T(8,128)} %get-tuple-element.665, s32[]{:T(128)} %get-tuple-element.663, f32[2,256,32,64]{1,3,2,0:T(8,128)} %get-tuple-element.583), kind=kLoop, calls=%fused_computation.45.clone.1 | loop fusion | bytes 8389120 | tf_op jit(solution)/shard_map/while/body/jit(dynamic_update_index_in_dim)/dynamic_update_slice | solution.py:131
  136.6 1.0 copy-done.6
  137.6 1.0 copy-done.5
  138.6 1.3 copy-done.7
  139.9 0.8 bitcast_dynamic-update-slice_fusion.16
  141.5 0.9 exp.51
  142.4 1.0 slice_reduce_fusion.3
  143.4 9.3 %all-gather.2 = f32[8,2,32]{2,1,0:T(2,128)S(1)} all-gather(f32[1,2,32]{2,1,0:T(2,128)S(1)} %bitcast.179), channel_id=2, replica_groups=mesh['tm'=8,'series'=4] {'tm'}, dimensions={0}, use_global_device_ids=true | all-gather | bytes 2304 | tf_op jit(solution)/shard_map/all_gather | solution.py:24
  152.7 78.0 %all-gather.5.cloned.1.call-done = f32[16,32,64,128]{3,2,1,0:T(8,128)} async-done(((f32[2,32,64,128]{3,2,1,0:T(8,128)}), f32[16,32,64,128]{3,2,1,0:T(8,128)}) %all-gather.5.cloned.1.call-update) | async-done | bytes 16777232 | tf_op jit(solution)/shard_map/all_gather | solution.py:24
  230.7 26.4 %while.49 = (s32[]{:T(128)}, f32[2,32,64,128]{3,2,1,0:T(8,128)}, s32[]{:T(128)}, f32[8,2,32]{2,1,0:T(2,128)S(1)}, f32[8,2,32,64,128]{4,3,2,1,0:T(8,128)}, /*index=5*/s32[]{:T(128)}, s32[]{:T(128)}) while((s32[]{:T(128)}, f32[2,32,64,128]{3,2,1,0:T(8,128)}, s32[]{:T(128)}, f32[8,2,32]{2,1,0:T(2,128)S(1)}, ...), condition=%wide.region_10.11_spmd.clone, body=%wide.region_9.10_spmd.clone.sunk | while | flops 2097156 | bytes 6292329 | solution.py:33
  230.7 3.2 fusion.55
  234.0 3.9 %fusion.55 = f32[2,32,64,128]{3,2,1,0:T(8,128)} fusion(f32[8,2,32,64,128]{4,3,2,1,0:T(8,128)} %get-tuple-element.713, s32[]{:T(128)} %get-tuple-element.702, f32[2,32,64,128]{3,2,1,0:T(8,128)} %get-tuple-element.703, f32[2,32]{1,0:T(2,128)S(1)} %exponential_bitcast_fusion.2, pred[]{:T(512)S(6)} %compare.6, pred[]{:T(512)S(6)} %lt.54), kind=kLoop, calls=%fused_computation.1.clone.1 | loop fusion | flops 2097152 | bytes 6291718 | tf_op jit(solution)/shard_map/while/body/eval_jaxpr/jit(_where)/select_n | solution.py:31
  237.8 3.9 %fusion.55 = f32[2,32,64,128]{3,2,1,0:T(8,128)} fusion(f32[8,2,32,64,128]{4,3,2,1,0:T(8,128)} %get-tuple-element.713, s32[]{:T(128)} %get-tuple-element.702, f32[2,32,64,128]{3,2,1,0:T(8,128)} %get-tuple-element.703, f32[2,32]{1,0:T(2,128)S(1)} %exponential_bitcast_fusion.2, pred[]{:T(512)S(6)} %compare.6, pred[]{:T(512)S(6)} %lt.54), kind=kLoop, calls=%fused_computation.1.clone.1 | loop fusion | flops 2097152 | bytes 6291718 | tf_op jit(solution)/shard_map/while/body/eval_jaxpr/jit(_where)/select_n | solution.py:31
  241.7 3.9 %fusion.55 = f32[2,32,64,128]{3,2,1,0:T(8,128)} fusion(f32[8,2,32,64,128]{4,3,2,1,0:T(8,128)} %get-tuple-element.713, s32[]{:T(128)} %get-tuple-element.702, f32[2,32,64,128]{3,2,1,0:T(8,128)} %get-tuple-element.703, f32[2,32]{1,0:T(2,128)S(1)} %exponential_bitcast_fusion.2, pred[]{:T(512)S(6)} %compare.6, pred[]{:T(512)S(6)} %lt.54), kind=kLoop, calls=%fused_computation.1.clone.1 | loop fusion | flops 2097152 | bytes 6291718 | tf_op jit(solution)/shard_map/while/body/eval_jaxpr/jit(_where)/select_n | solution.py:31
  245.5 3.9 %fusion.55 = f32[2,32,64,128]{3,2,1,0:T(8,128)} fusion(f32[8,2,32,64,128]{4,3,2,1,0:T(8,128)} %get-tuple-element.713, s32[]{:T(128)} %get-tuple-element.702, f32[2,32,64,128]{3,2,1,0:T(8,128)} %get-tuple-element.703, f32[2,32]{1,0:T(2,128)S(1)} %exponential_bitcast_fusion.2, pred[]{:T(512)S(6)} %compare.6, pred[]{:T(512)S(6)} %lt.54), kind=kLoop, calls=%fused_computation.1.clone.1 | loop fusion | flops 2097152 | bytes 6291718 | tf_op jit(solution)/shard_map/while/body/eval_jaxpr/jit(_where)/select_n | solution.py:31
  249.4 3.9 %fusion.55 = f32[2,32,64,128]{3,2,1,0:T(8,128)} fusion(f32[8,2,32,64,128]{4,3,2,1,0:T(8,128)} %get-tuple-element.713, s32[]{:T(128)} %get-tuple-element.702, f32[2,32,64,128]{3,2,1,0:T(8,128)} %get-tuple-element.703, f32[2,32]{1,0:T(2,128)S(1)} %exponential_bitcast_fusion.2, pred[]{:T(512)S(6)} %compare.6, pred[]{:T(512)S(6)} %lt.54), kind=kLoop, calls=%fused_computation.1.clone.1 | loop fusion | flops 2097152 | bytes 6291718 | tf_op jit(solution)/shard_map/while/body/eval_jaxpr/jit(_where)/select_n | solution.py:31
  253.3 3.9 %fusion.55 = f32[2,32,64,128]{3,2,1,0:T(8,128)} fusion(f32[8,2,32,64,128]{4,3,2,1,0:T(8,128)} %get-tuple-element.713, s32[]{:T(128)} %get-tuple-element.702, f32[2,32,64,128]{3,2,1,0:T(8,128)} %get-tuple-element.703, f32[2,32]{1,0:T(2,128)S(1)} %exponential_bitcast_fusion.2, pred[]{:T(512)S(6)} %compare.6, pred[]{:T(512)S(6)} %lt.54), kind=kLoop, calls=%fused_computation.1.clone.1 | loop fusion | flops 2097152 | bytes 6291718 | tf_op jit(solution)/shard_map/while/body/eval_jaxpr/jit(_where)/select_n | solution.py:31
  257.1 9.9 %multiply_add_fusion = f32[2,2,256,32,64]{2,4,3,1,0:T(8,128)} fusion(f32[2,2,256,32,64]{2,4,3,1,0:T(8,128)} %get-tuple-element.742, f32[2,2,256,32]{2,3,1,0:T(8,128)S(1)} %exp.51, bf16[2,2,256,128,1]{3,2,4,1,0:T(8,128)(2,1)} %bitcast.15, f32[2,2,32,64,128]{4,3,2,1,0:T(8,128)} %get-tuple-element.744, f32[2,32,64,128]{3,2,1,0:T(8,128)} %get-tuple-element.222, ...), kind=kOutput, calls=%fused_computation.59 | convolution fusion | flops 544210944 | bytes 23462400 | tf_op jit(solution)/shard_map/sctn,schpn->scthp/dot_general | solution.py:153
  267.0 16.2 %copy.68 = f32[2,2,256,32,64]{4,3,2,1,0:T(8,128)} copy(f32[2,2,256,32,64]{2,4,3,1,0:T(8,128)} %multiply_add_fusion) | data formatting | bytes 16777216 | tf_op jit(solution)/shard_map/reshape | solution.py:155
  283.2 14.8 %reshape.172 = f32[1024,2048]{1,0:T(8,128)} reshape(f32[2,2,256,32,64]{4,3,2,1,0:T(8,128)} %copy.68) | data formatting | bytes 16777216 | tf_op jit(solution)/shard_map/reshape | solution.py:155
  298.0 11.5 %multiply_reduce_fusion = (f32[1024]{0:T(1024)S(1)}, f32[1024,2048]{1,0:T(8,128)}) fusion(f32[1024,2048]{1,0:T(8,128)} %reshape.172, bf16[1024,1024]{1,0:T(8,128)(2,1)S(1)} %bitcast.172, bf16[1024,2048]{1,0:T(8,128)(2,1)} %param.20), kind=kOutput, calls=%fused_computation.57 | convolution fusion | flops 4309646336 | bytes 23072768 | tf_op jit(solution)/shard_map/dot_general | solution.py:70
  309.6 8.0 %fusion.30 = f32[1024,1024]{1,0:T(8,128)S(1)} fusion(bf16[2048,1024]{1,0:T(8,128)(2,1)S(1)} %copy-done.17, f32[2048]{0:T(1024)S(1)} %copy-done.18, f32[1024]{0:T(1024)S(1)} %add_rsqrt_fusion, f32[1024,2048]{1,0:T(8,128)S(1)} %copy-done.2, f32[1024,2048]{1,0:T(8,128)} %get-tuple-element.400), kind=kOutput, calls=%fused_computation.68 | convolution fusion | flops 4311744512 | bytes 25178112 | tf_op jit(solution)/shard_map/dot_general | solution.py:159
  317.6 1.6 multiply_convert_fusion.8
  (147 shorter events, 12.7 us)
Async XLA Ops:
  6.5 1.6 copy-start
  6.5 224.2 %all-gather.5.cloned.1.call-start = ((), (), s32[]{:S(2)}) async-start(), calls=%async_computation | async-start | bytes 18874368 | tf_op jit(solution)/shard_map/all_gather | solution.py:24
  8.1 12.3 %copy-start.22 = (u32[32]{0:T(128)S(1)}, u32[32]{0:T(128)}, u32[]{:S(2)}) copy-start(u32[32]{0:T(128)} %constant.109) | copy-start | bytes 388
  8.1 13.6 %copy-start.19 = (s32[2]{0:T(128)S(1)}, s32[2]{0:T(128)}, u32[]{:S(2)}) copy-start(s32[2]{0:T(128)} %param.30) | copy-start | bytes 28
  8.1 23.1 %copy-start.20 = (s32[2]{0:T(128)S(1)}, s32[2]{0:T(128)}, u32[]{:S(2)}) copy-start(s32[2]{0:T(128)} %param.31) | copy-start | bytes 28
  8.1 23.4 %copy-start.11 = (bf16[1024,32]{0,1:T(8,128)(2,1)S(1)}, bf16[1024,32]{0,1:T(8,128)(2,1)}, u32[]{:S(2)}) copy-start(bf16[1024,32]{0,1:T(8,128)(2,1)} %param.22) | copy-start | bytes 196612
  8.1 23.4 %copy-start.16 = (f32[32]{0:T(128)S(1)}, f32[32]{0:T(128)}, u32[]{:S(2)}) copy-start(f32[32]{0:T(128)} %param.25) | copy-start | bytes 388
  8.1 24.2 %copy-start.12 = (f32[4,2304]{1,0:T(4,128)S(1)}, f32[4,2304]{1,0:T(4,128)}, u32[]{:S(2)}) copy-start(f32[4,2304]{1,0:T(4,128)} %param.23) | copy-start | bytes 110596
  15.8 2.2 copy-start.3
  18.0 21.8 %collective-permute-start = (bf16[2,3,2304]{2,0,1:T(2,128)(2,1)S(1)}, bf16[2,3,2304]{2,0,1:T(2,128)(2,1)S(1)}, u32[]{:S(2)}, u32[]{:S(2)}) collective-permute-start(bf16[2,3,2304]{2,0,1:T(2,128)(2,1)S(1)} %copy.72), channel_id=1, source_target_pairs={{0,4},{4,8},{8,12},{12,16},{16,20},{20,24},{24,28},{1,5},{5,9},{9,... | collective-permute-start | bytes 82952 | tf_op jit(solution)/shard_map/ppermute | solution.py:19
  31.5 0.8 copy-start.13
  32.4 8.1 %copy-start.15 = (f32[2304]{0:T(1024)S(1)}, f32[2304]{0:T(1024)}, u32[]{:S(2)}) copy-start(f32[2304]{0:T(1024)} %param.24) | copy-start | bytes 27652
  57.2 8.6 %copy-start.8 = (f32[32]{0:T(128)S(1)}, f32[32]{0:T(128)}, u32[]{:S(2)}) copy-start(f32[32]{0:T(128)} %param.26) | copy-start | bytes 388
  57.2 8.6 %copy-start.21 = (f32[32]{0:T(128)S(1)}, f32[32]{0:T(128)}, u32[]{:S(2)}) copy-start(f32[32]{0:T(128)} %param.27) | copy-start | bytes 388
  93.5 5.0 %copy-start.1 = (f32[2,32,64,128]{3,2,1,0:T(8,128)S(1)}, f32[2,32,64,128]{3,2,1,0:T(8,128)}, u32[]{:S(2)}) copy-start(f32[2,32,64,128]{3,2,1,0:T(8,128)} %get-tuple-element.585) | copy-start | bytes 6291460 | tf_op jit(solution)/shard_map/while
  93.5 5.0 %copy-start.4 = (f32[2,2,32,64,128]{4,3,2,1,0:T(8,128)S(1)}, f32[2,2,32,64,128]{4,3,2,1,0:T(8,128)}, u32[]{:S(2)}) copy-start(f32[2,2,32,64,128]{4,3,2,1,0:T(8,128)} %get-tuple-element.667) | copy-start | bytes 12582916 | tf_op jit(solution)/shard_map/while
  93.5 6.2 %copy-start.6 = (f32[2,32,64,128]{3,2,1,0:T(8,128)S(1)}, f32[2,32,64,128]{3,2,1,0:T(8,128)}, u32[]{:S(2)}) copy-start(f32[2,32,64,128]{3,2,1,0:T(8,128)} %get-tuple-element.664) | copy-start | bytes 6291460 | tf_op jit(solution)/shard_map/while
  98.5 3.6 %copy-start.9 = (f32[2,2,256,32]{2,3,1,0:T(8,128)S(1)}, f32[2,2,256,32]{2,3,1,0:T(8,128)}, u32[]{:S(2)}) copy-start(f32[2,2,256,32]{2,3,1,0:T(8,128)} %get-tuple-element.666) | copy-start | bytes 393220 | tf_op jit(solution)/shard_map/while
  98.8 2.0 copy-start.5
  100.8 1.3 copy-start.7
  103.0 0.7 copy-start.10
  131.3 5.0 %copy-start.1 = (f32[2,32,64,128]{3,2,1,0:T(8,128)S(1)}, f32[2,32,64,128]{3,2,1,0:T(8,128)}, u32[]{:S(2)}) copy-start(f32[2,32,64,128]{3,2,1,0:T(8,128)} %get-tuple-element.585) | copy-start | bytes 6291460 | tf_op jit(solution)/shard_map/while
  131.3 5.0 %copy-start.4 = (f32[2,2,32,64,128]{4,3,2,1,0:T(8,128)S(1)}, f32[2,2,32,64,128]{4,3,2,1,0:T(8,128)}, u32[]{:S(2)}) copy-start(f32[2,2,32,64,128]{4,3,2,1,0:T(8,128)} %get-tuple-element.667) | copy-start | bytes 12582916 | tf_op jit(solution)/shard_map/while
  131.3 6.2 %copy-start.6 = (f32[2,32,64,128]{3,2,1,0:T(8,128)S(1)}, f32[2,32,64,128]{3,2,1,0:T(8,128)}, u32[]{:S(2)}) copy-start(f32[2,32,64,128]{3,2,1,0:T(8,128)} %get-tuple-element.664) | copy-start | bytes 6291460 | tf_op jit(solution)/shard_map/while
  136.3 3.6 %copy-start.9 = (f32[2,2,256,32]{2,3,1,0:T(8,128)S(1)}, f32[2,2,256,32]{2,3,1,0:T(8,128)}, u32[]{:S(2)}) copy-start(f32[2,2,256,32]{2,3,1,0:T(8,128)} %get-tuple-element.666) | copy-start | bytes 393220 | tf_op jit(solution)/shard_map/while
  136.5 2.0 copy-start.5
  138.6 1.3 copy-start.7
  140.8 0.7 copy-start.10
  298.0 11.5 %copy-start.2 = (f32[1024,2048]{1,0:T(8,128)S(1)}, f32[1024,2048]{1,0:T(8,128)}, u32[]{:S(2)}) copy-start(f32[1024,2048]{1,0:T(8,128)} %reshape.172) | copy-start | bytes 25165828
  298.0 11.5 %copy-start.17 = (bf16[2048,1024]{1,0:T(8,128)(2,1)S(1)}, bf16[2048,1024]{1,0:T(8,128)(2,1)}, u32[]{:S(2)}) copy-start(bf16[2048,1024]{1,0:T(8,128)(2,1)} %param.29) | copy-start | bytes 12582916
  298.0 11.5 %copy-start.18 = (f32[2048]{0:T(1024)S(1)}, f32[2048]{0:T(1024)}, u32[]{:S(2)}) copy-start(f32[2048]{0:T(1024)} %param.28) | copy-start | bytes 24580
  309.6 8.0 %copy-start.14 = (f32[2,512]{1,0:T(2,128)S(1)}, f32[2,512]{1,0:T(2,128)}, u32[]{:S(2)}) copy-start(f32[2,512]{1,0:T(2,128)} %copy-done.13) | copy-start | bytes 12292
Sparse Core Ops, SparseCore 0:
  141.6 89.1 all-gather.4
where the time goes:
time: 328 us; the launch traced here: 326 us
  local copies, waits for them, and re-layouts  91.1 us (28%)
  waiting for transfers between devices  78 us (24%)
  matrix products  67 us (20%)
  other arithmetic  54.3 us (17%)
  blocking collectives  18.6 us (6%)
  between operations  14.3 us (4%)
    all_gather x1, waiting for transfers between devices, carried_in(): pieces = jax.tree.map(lambda part: lax.all_gather(part, axis), value)  78 us
    reshape x2, local copies, waits for them, and re-layouts, body(): outputs = outputs.reshape(series_here * local_steps, DI)  31.1 us
    select_n x7, other arithmetic, step(): jnp.where(position < mine, new, old)  26.3 us
    dot_general x4, matrix products, block_terms(): jnp.einsum('hts,shp->thp', weights, inputs_x, preferred_element_type=jnp....  21.4 us
    another operation x20, other arithmetic  17.2 us
    dynamic_update_slice x8, local copies, waits for them, and re-layouts, body(): lax.map(series_pass, (inputs_x, inputs_b, inputs_c, step_sizes, block_live))  12.4 us
    dynamic_slice x8, local copies, waits for them, and re-layouts, body(): lax.map(series_pass, (inputs_x, inputs_b, inputs_c, step_sizes, block_live))  11.8 us
    dot_general x1, matrix products, body(): gate = jnp.dot(flat_tokens, gate_proj, preferred_element_type=jnp.float32)  11.5 us
  transfers between devices with their start and end apart: 2, of which 1 were waited for; matrix products, arithmetic and copies ran while one was open for 3% of the time, Pallas kernels for 0%

commit v1 on v0

v1 whole, which is shorter than its diff:
```python
import functools

import jax
import jax.numpy as jnp
from jax import lax
from jax.experimental import pallas as pl
from jax.experimental.pallas import tpu as pltpu
from jax.sharding import PartitionSpec as P

BLOCK = 256
CHUNK = 256
LANES = 128
TAIL = 16
EPSILON = 1e-05
F32 = jnp.float32
BF16 = jnp.bfloat16
VMEM_LIMIT = 60 * 1024 * 1024


def dot(a, b):
    return jnp.dot(a, b, preferred_element_type=F32)


def three_parts(value):
    high = value.astype(BF16)
    rest = value - high.astype(F32)
    mid = rest.astype(BF16)
    low = (rest - mid.astype(F32)).astype(BF16)
    return high, mid, low


def lane_parts(value, heads):
    high, mid, low = three_parts(value)
    group = lax.broadcasted_iota(jnp.int32, value.shape, 1) // heads
    picked = jnp.where(
        group == 0, high.astype(F32), jnp.where(group == 1, mid.astype(F32), low.astype(F32))
    )
    return picked.astype(BF16)


def silu(value):
    half = 0.5 * value
    return half + half * jnp.tanh(half)


def scan_kernel(
    heads,
    remaining,
    tok_ref,
    rim_ref,
    w_ref,
    wstep_ref,
    ck_ref,
    cb_ref,
    sb_ref,
    dr_ref,
    e_ref,
    x_ref,
    bc_ref,
    ec_ref,
    ed_ref,
    cum_ref,
    rt_ref,
    before_ref,
    end_ref,
    raw,
):
    steps = tok_ref.shape[1]
    width = w_ref.shape[1]
    inner = e_ref.shape[1]
    blocks = steps // BLOCK
    taps = ck_ref.shape[0]
    series = pl.program_id(0)
    tokens = tok_ref[0]
    rim = rim_ref[0]

    def convolved(slot, start):
        cols = slice(start, start + CHUNK)
        weights = w_ref[:, cols]
        raw[slot, 0:TAIL, :] = dot(rim, weights).astype(BF16).astype(F32)
        raw[slot, TAIL:, :] = dot(tokens, weights).astype(BF16).astype(F32)
        total = cb_ref[:, cols] + jnp.zeros((steps, CHUNK), F32)
        for tap in range(taps):
            first = TAIL - (taps - 1) + tap
            total = total + ck_ref[tap : tap + 1, cols] * raw[slot, first : first + steps, :]
        return silu(total).astype(BF16)

    bc = convolved(0, inner)
    bc_ref[0] = bc

    step_raw = dot(tokens, wstep_ref[...]) + sb_ref[...]
    soft = jnp.maximum(step_raw, 0.0) + jnp.log1p(jnp.exp(-jnp.abs(step_raw)))
    row = lax.broadcasted_iota(jnp.int32, soft.shape, 0)
    soft = jnp.where(row < remaining[series], soft, 0.0)
    drop = -soft * dr_ref[...]
    below = (
        lax.broadcasted_iota(jnp.int32, (BLOCK, BLOCK), 0)
        >= lax.broadcasted_iota(jnp.int32, (BLOCK, BLOCK), 1)
    ).astype(F32).astype(BF16)
    offset = jnp.zeros((1, LANES), F32)
    weight_parts, decay_rows, b_rows = [], [], []
    for block in range(blocks):
        rows = slice(block * BLOCK, (block + 1) * BLOCK)
        high, mid, low = three_parts(drop[rows])
        cum = dot(below, high) + dot(below, mid) + dot(below, low)
        last = cum[BLOCK - 1 : BLOCK]
        cum_ref[0, rows, :] = cum
        ec_ref[0, rows, :] = lane_parts(jnp.exp(cum), heads)
        ed_ref[0, rows, :] = lane_parts(jnp.exp(cum + offset), heads)
        offset = offset + last
        rt_ref[0, block] = (cum - jnp.log(soft[rows])).T[:heads]
        weight_parts.append(lane_parts(jnp.exp(last - cum) * soft[rows], heads))
        decay_rows.append(lane_parts(jnp.exp(last) + jnp.zeros((TAIL, LANES), F32), heads))
        b_rows.append(bc[rows, :LANES].astype(F32).T.astype(BF16))
    device_row = lane_parts(jnp.exp(offset) + jnp.zeros((TAIL, LANES), F32), heads)

    states = bc.shape[1] // 2
    for index, start in enumerate(range(0, inner, CHUNK)):
        cols = slice(start, start + CHUNK)
        x = convolved((index + 1) % 2, start)
        x_ref[0, :, cols] = x
        state = None
        for block in range(blocks):
            rows = slice(block * BLOCK, (block + 1) * BLOCK)
            wide = dot(weight_parts[block], e_ref[:, cols])
            weighted = (x[rows].astype(F32) * wide).astype(BF16)
            added = dot(b_rows[block], weighted)
            if state is None:
                state = added
            else:
                before_ref[0, block - 1, :, cols] = state.astype(BF16)
                state = dot(decay_rows[block], e_ref[:, cols])[0:1] * state + added
        end_ref[0, 0:states, cols] = state.astype(BF16)
        decay = dot(device_row, e_ref[:, cols])
        high, mid, low = (part.astype(F32) for part in three_parts(decay))
        place = lax.broadcasted_iota(jnp.int32, decay.shape, 0)
        packed = jnp.where(place == 0, high, jnp.where(place == 1, mid, jnp.where(place == 2, low, 0.0)))
        end_ref[0, states:, cols] = packed.astype(BF16)


def within_kernel(heads, x_ref, bc_ref, ec_ref, cum_ref, rt_ref, before_ref, skip_ref, e_ref, out_ref):
    inner = x_ref.shape[2]
    head_size = inner // heads
    here = pl.program_id(1)
    half = BLOCK // 2
    b_part = bc_ref[0, :, :LANES]
    c_part = bc_ref[0, :, LANES:]
    scores = lax.dot_general(c_part, b_part, (((1,), (1,)), ((), ())), preferred_element_type=F32)
    corner = lax.broadcasted_iota(jnp.int32, (half, half), 0) >= lax.broadcasted_iota(
        jnp.int32, (half, half), 1
    )
    earlier = jnp.where(here > 0, c_part.astype(F32), 0.0).astype(BF16)
    cum = cum_ref[0]
    ec = ec_ref[0]
    empty = jnp.zeros((half, half), BF16)
    lane_head = lax.broadcasted_iota(jnp.int32, (BLOCK, CHUNK), 1) // head_size
    for start in range(0, inner, CHUNK):
        cols = slice(start, start + CHUNK)
        x = x_ref[0, :, cols]
        x_wide = x.astype(F32)
        base = skip_ref[:, cols] * x_wide + dot(ec, e_ref[:, cols]) * dot(earlier, before_ref[0, 0, :, cols])
        lefts, rights = [], []
        for local in range(CHUNK // head_size):
            head = start // head_size + local
            at = cum[:, head : head + 1]
            of = rt_ref[0, 0, head : head + 1, :]
            first = jnp.where(corner, jnp.exp(jnp.where(corner, at[:half] - of[:, :half], 0.0)), 0.0)
            middle = jnp.exp(at[half:] - of[:, :half])
            last = jnp.where(corner, jnp.exp(jnp.where(corner, at[half:] - of[:, half:], 0.0)), 0.0)
            top = (first * scores[:half, :half]).astype(BF16)
            left = (middle * scores[half:, :half]).astype(BF16)
            right = (last * scores[half:, half:]).astype(BF16)
            lefts.append(
                jnp.concatenate(
                    [
                        jnp.concatenate([top, empty], axis=1),
                        jnp.concatenate([left, right], axis=1),
                    ],
                    axis=0,
                )
            )
            rights.append(jnp.where(lane_head == local, x_wide, 0.0).astype(BF16))
        mixed = dot(jnp.concatenate(lefts, axis=1), jnp.concatenate(rights, axis=0))
        out_ref[0, :, cols] = (mixed + base).astype(out_ref.dtype)


def out_kernel(
    remaining,
    tok_ref,
    gp_ref,
    part_ref,
    bc_ref,
    ed_ref,
    sin_ref,
    gain_ref,
    op_ref,
    e_ref,
    out_ref,
    gated,
):
    steps = tok_ref.shape[1]
    inner = gp_ref.shape[1]
    series = pl.program_id(0)
    tokens = tok_ref[0]
    c_part = bc_ref[0, :, LANES:]
    ed = ed_ref[0]
    squares = jnp.zeros((steps, LANES), F32)
    for start in range(0, inner, CHUNK):
        cols = slice(start, start + CHUNK)
        gate = dot(tokens, gp_ref[:, cols])
        inter = dot(ed, e_ref[:, cols]) * dot(c_part, sin_ref[0, :, cols])
        value = (part_ref[0, :, cols].astype(F32) + inter) * silu(gate)
        gated[:, cols] = value
        square = value * value
        for lane in range(0, CHUNK, LANES):
            squares = squares + square[:, lane : lane + LANES]
    mean = jnp.sum(squares, axis=1, keepdims=True) / inner
    scale = lax.rsqrt(mean + EPSILON)
    normed = (gated[...] * scale * gain_ref[...]).astype(BF16)
    row = lax.broadcasted_iota(jnp.int32, (steps, CHUNK), 0)
    live = row < remaining[series]
    for start in range(0, op_ref.shape[1], CHUNK):
        cols = slice(start, start + CHUNK)
        result = dot(normed, op_ref[:, cols])
        out_ref[0, :, cols] = jnp.where(live, result, 0.0).astype(BF16)


def whole(shape):
    return pl.BlockSpec(shape, lambda *_: (0,) * len(shape))


def per_series(shape):
    return pl.BlockSpec((1,) + shape, lambda s, *_: (s,) + (0,) * len(shape))


def unpack(packed):
    states = packed.shape[0] - TAIL
    tail = packed[states : states + 3].astype(F32)
    return jnp.sum(tail, axis=0, keepdims=True), packed[:states].astype(F32)


def pack(decay, state):
    high = lax.reduce_precision(decay, 8, 7)
    rest = decay - high
    mid = lax.reduce_precision(rest, 8, 7)
    low = rest - mid
    filler = jnp.zeros((TAIL - 3, decay.shape[1]), F32)
    return jnp.concatenate([state, high, mid, low, filler], axis=0).astype(BF16)


def incoming_state(packed, axis):
    count, mine = lax.axis_size(axis), lax.axis_index(axis)
    half = packed.shape[1] // 2
    odd = mine % 2 == 1
    left, right = packed[:, :half], packed[:, half:]
    swap = [(i, i ^ 1) for i in range(count)]
    own = jnp.where(odd, right, left)
    got = lax.ppermute(jnp.where(odd, left, right), axis, swap)
    first = unpack(jnp.where(odd, got, own))
    second = unpack(jnp.where(odd, own, got))
    total = (first[0] * second[0], second[0] * first[1] + second[1])
    prefix_decay, prefix = jnp.ones_like(first[0]), jnp.zeros_like(first[1])
    bit = 2
    while bit < count:
        final = bit * 2 >= count
        pairs = [(i, i ^ bit) for i in range(count) if not final or not i & bit]
        other = unpack(lax.ppermute(pack(*total), axis, pairs))
        later = (mine & bit) != 0
        prefix = jnp.where(later, prefix_decay * other[1] + prefix, prefix)
        prefix_decay = jnp.where(later, prefix_decay * other[0], prefix_decay)
        if not final:
            total = (
                total[0] * other[0],
                jnp.where(later, total[0] * other[1] + total[1], other[0] * total[1] + other[1]),
            )
        bit *= 2
    behind = (first[0] * prefix + first[1]).astype(BF16)
    prefix = prefix.astype(BF16)
    here = jnp.where(odd, behind, prefix)
    there = lax.ppermute(jnp.where(odd, prefix, behind), axis, swap)
    return jnp.concatenate([jnp.where(odd, there, here), jnp.where(odd, here, there)], axis=1)


def params():
    return pltpu.CompilerParams(vmem_limit_bytes=VMEM_LIMIT)


def body(
    tokens,
    gate_proj,
    input_proj,
    step_proj,
    conv_kernel,
    conv_bias,
    step_bias,
    decay_rate,
    skip_gain,
    norm_gain,
    out_proj,
    lengths,
    slot_series,
):
    series, steps, model = tokens.shape
    inner = gate_proj.shape[1]
    width = input_proj.shape[1]
    states = (width - inner) // 2
    heads = step_bias.shape[0]
    head_size = inner // heads
    blocks = steps // BLOCK
    copies = LANES // heads
    tm, groups = lax.axis_size("tm"), lax.axis_size("series")
    place = lax.axis_index("series")

    taps = conv_kernel.shape[0]
    rim = lax.ppermute(tokens[:, steps - TAIL :], "tm", [(i, i + 1) for i in range(tm - 1)])
    my_lengths = jnp.zeros_like(lengths)
    for shift in range(groups):
        held = lengths
        if shift:
            held = lax.ppermute(lengths, "series", [(i, (i + shift) % groups) for i in range(groups)])
        number = ((place - shift) % groups) * series + jnp.arange(series, dtype=jnp.int32)
        matches = slot_series[:, None] == number[None, :]
        my_lengths = my_lengths + jnp.sum(jnp.where(matches, held[None, :], 0), axis=1)
    remaining = my_lengths - lax.axis_index("tm") * steps

    lane = jnp.arange(LANES)[:, None]
    column = jnp.arange(inner)[None, :]
    expand = ((lane % heads == column // head_size) & (lane < 3 * heads)).astype(BF16)
    step_wide = jnp.tile(step_proj, (1, copies))
    bias_wide = jnp.tile(step_bias, copies)[None]
    rate_wide = jnp.tile(decay_rate, copies)[None]
    skip_wide = jnp.repeat(skip_gain, head_size)[None]

    smem = pl.BlockSpec(memory_space=pltpu.SMEM)
    x, bc, ec, ed, cum, rt, before, end = pl.pallas_call(
        functools.partial(scan_kernel, heads),
        grid=(series,),
        in_specs=[
            smem,
            per_series((steps, model)),
            per_series((TAIL, model)),
            whole((model, width)),
            whole((model, LANES)),
            whole((taps, width)),
            whole((1, width)),
            whole((1, LANES)),
            whole((1, LANES)),
            whole((LANES, inner)),
        ],
        out_specs=[
            per_series((steps, inner)),
            per_series((steps, width - inner)),
            per_series((steps, LANES)),
            per_series((steps, LANES)),
            per_series((steps, LANES)),
            per_series((blocks, heads, BLOCK)),
            per_series((max(blocks - 1, 1), states, inner)),
            per_series((states + TAIL, inner)),
        ],
        out_shape=[
            jax.ShapeDtypeStruct((series, steps, inner), BF16),
            jax.ShapeDtypeStruct((series, steps, width - inner), BF16),
            jax.ShapeDtypeStruct((series, steps, LANES), BF16),
            jax.ShapeDtypeStruct((series, steps, LANES), BF16),
            jax.ShapeDtypeStruct((series, steps, LANES), F32),
            jax.ShapeDtypeStruct((series, blocks, heads, BLOCK), F32),
            jax.ShapeDtypeStruct((series, max(blocks - 1, 1), states, inner), BF16),
            jax.ShapeDtypeStruct((series, states + TAIL, inner), BF16),
        ],
        scratch_shapes=[pltpu.VMEM((2, steps + TAIL, CHUNK), F32)],
        compiler_params=params(),
        cost_estimate=pl.CostEstimate(
            flops=2 * series * steps * model * width, bytes_accessed=16 << 20, transcendentals=0
        ),
        name="scan_terms",
    )(
        remaining,
        tokens,
        rim,
        input_proj,
        step_wide,
        conv_kernel,
        conv_bias[None],
        bias_wide,
        rate_wide,
        expand,
    )

    incoming = jnp.stack([incoming_state(end[s], "tm") for s in range(series)])

    def per_block(shape):
        return pl.BlockSpec((1, BLOCK) + shape, lambda s, b: (s, b) + (0,) * len(shape))

    partial = pl.pallas_call(
        functools.partial(within_kernel, heads),
        grid=(series, blocks),
        in_specs=[
            per_block((inner,)),
            per_block((width - inner,)),
            per_block((LANES,)),
            per_block((LANES,)),
            pl.BlockSpec((1, 1, heads, BLOCK), lambda s, b: (s, b, 0, 0)),
            pl.BlockSpec((1, 1, states, inner), lambda s, b: (s, jnp.maximum(b - 1, 0), 0, 0)),
            whole((1, inner)),
            whole((LANES, inner)),
        ],
        out_specs=per_block((inner,)),
        out_shape=jax.ShapeDtypeStruct((series, steps, inner), BF16),
        compiler_params=params(),
        cost_estimate=pl.CostEstimate(
            flops=16 * series * steps * BLOCK * inner, bytes_accessed=16 << 20, transcendentals=0
        ),
        name="within_blocks",
    )(x, bc, ec, cum, rt, before, skip_wide, expand)

    return pl.pallas_call(
        out_kernel,
        grid=(series,),
        in_specs=[
            smem,
            per_series((steps, model)),
            whole((model, inner)),
            per_series((steps, inner)),
            per_series((steps, width - inner)),
            per_series((steps, LANES)),
            per_series((states, inner)),
            whole((1, inner)),
            whole((inner, model)),
            whole((LANES, inner)),
        ],
        out_specs=per_series((steps, model)),
        out_shape=jax.ShapeDtypeStruct((series, steps, model), BF16),
        scratch_shapes=[pltpu.VMEM((steps, inner), F32)],
        compiler_params=params(),
        cost_estimate=pl.CostEstimate(
            flops=4 * series * steps * model * inner, bytes_accessed=20 << 20, transcendentals=0
        ),
        name="gate_and_out",
    )(remaining, tokens, gate_proj, partial, bc, ed, incoming, norm_gain[None], out_proj, expand)


def solution(mesh):
    in_specs = (P("series", "tm", None),) + (P(),) * 10 + (P("series"), P("series"))
    return jax.shard_map(
        body, mesh=mesh, in_specs=in_specs, out_specs=P("series", "tm", None), check_vma=False
    )
```

time: 328 us -> 114 us (0.35)
  local copies, waits for them, and re-layouts: 91.1 us -> 10.9 us
  matrix products: 67 us -> 0 us
  waiting for transfers between devices: 78 us -> 15.8 us
  Pallas kernels: 0 us -> 61.7 us
  other arithmetic: 54.3 us -> 5.15 us
  blocking collectives: 18.6 us -> 0 us
  starting transfers between devices: 2.4 us -> 19.8 us
  between operations: 14.3 us -> 0.43 us
    all_gather x1 -> x0, waiting for transfers between devices: 78 us -> none  [carried_in(): pieces = jax.tree.map(lambda part: lax.all_gather(part, axis), value)]
    dot_general x17 -> x0, matrix products: 67 us -> none  [the longest x4 21.4 us: block_terms(): jnp.einsum('hts,shp->thp', weights, inputs_x, preferred_element_type=jnp....]
    pallas_call x0 -> x3, Pallas kernels: none -> 61.7 us  [the longest x1 29.5 us: body(): pl.pallas_call(functools.partial(scan_kernel, heads), grid=(series,), in_...]
    reshape x5 -> x0, local copies, waits for them, and re-layouts: 45.3 us -> none  [the longest x2 31.1 us: body(): outputs = outputs.reshape(series_here * local_steps, DI)]
    select_n x7 -> x12, other arithmetic: 26.3 us -> 0.73 us  [the longest x2 0.44 us: incoming_state(): there = lax.ppermute(jnp.where(odd, prefix, behind), axis, swap)]
    ppermute x1 -> x12, starting transfers between devices: 2.4 us -> 19.8 us  [the longest x4 9.05 us: incoming_state(): other = unpack(lax.ppermute(pack(*total), axis, pairs))]
    ppermute x1 -> x12, waiting for transfers between devices: 0.01 us -> 15.8 us  [the longest x4 14.4 us: incoming_state(): other = unpack(lax.ppermute(pack(*total), axis, pairs))]
    another operation x21 -> x11, other arithmetic: 17.3 us -> 1.77 us  [the longest x3 1.16 us: body(): incoming = jnp.stack([incoming_state(end[s], 'tm') for s in range(series)])]
  transfers between devices with their start and end apart: 2 -> 12, of which waited for: 1 -> 4; matrix products, arithmetic and copies ran while one was open for 3% -> 11% of each run, Pallas kernels for 0% -> 12%
where the time goes in v1:
time: 114 us
  Pallas kernels  61.7 us (54%)
  starting transfers between devices  19.8 us (17%)
  waiting for transfers between devices  15.8 us (14%)
  local copies, waits for them, and re-layouts  10.9 us (10%)
  other arithmetic  5.15 us (5%)
    pallas_call x1, Pallas kernels, body(): pl.pallas_call(functools.partial(scan_kernel, heads), grid=(series,), in_...  29.5 us
    pallas_call x1, Pallas kernels, body(): pl.pallas_call(out_kernel, grid=(series,), in_specs=[smem, per_series((st...  18.5 us
    ppermute x4, waiting for transfers between devices, incoming_state(): other = unpack(lax.ppermute(pack(*total), axis, pairs))  14.4 us
    pallas_call x1, Pallas kernels, body(): pl.pallas_call(functools.partial(within_kernel, heads), grid=(series, blo...  13.7 us
    ppermute x4, starting transfers between devices, incoming_state(): other = unpack(lax.ppermute(pack(*total), axis, pairs))  9.05 us
    ppermute x3, starting transfers between devices, body(): lax.ppermute(lengths, 'series', [(i, (i + shift) % groups) for i in range...  6.99 us
    ppermute x2, starting transfers between devices, incoming_state(): got = lax.ppermute(jnp.where(odd, left, right), axis, swap)  2.37 us
  transfers between devices with their start and end apart: 12, of which 4 were waited for; matrix products, arithmetic and copies ran while one was open for 11% of the time, Pallas kernels for 12%

profile of v1, /device:TPU:0, one launch (start us, length us, event | category | flops | bytes accessed | tf_op | source)
XLA Modules:
  0.0 113.9 jit_solution(2304410380694265850)
XLA Ops:
  0.0 3.1 %collective-permute-start = (s32[2]{0:T(128)}, s32[2]{0:T(128)S(1)}, u32[]{:S(2)}, u32[]{:S(2)}) collective-permute-start(s32[2]{0:T(128)} %param.24), channel_id=1, source_target_pairs={{0,1},{1,2},{2,3},{3,0},{4,5},{5,6},{6,7},{7,4},{8,9},{9,10},{10,1... | collective-permute-start | bytes 32 | tf_op jit(solution)/shard_map/ppermute | solution.py:320
  3.1 2.6 %collective-permute-start.1 = (s32[2]{0:T(128)}, s32[2]{0:T(128)S(1)}, u32[]{:S(2)}, u32[]{:S(2)}) collective-permute-start(s32[2]{0:T(128)} %param.24), channel_id=1, source_target_pairs={{0,2},{1,3},{2,0},{3,1},{4,6},{5,7},{6,4},{7,5},{8,10},{9,11},{10,... | collective-permute-start | bytes 32 | tf_op jit(solution)/shard_map/ppermute | solution.py:320
  5.6 1.3 %collective-permute-start.2 = (s32[2]{0:T(128)}, s32[2]{0:T(128)S(1)}, u32[]{:S(2)}, u32[]{:S(2)}) collective-permute-start(s32[2]{0:T(128)} %param.24), channel_id=1, source_target_pairs={{0,3},{1,0},{2,1},{3,2},{4,7},{5,4},{6,5},{7,6},{8,11},{9,8},{10,9... | collective-permute-start | bytes 32 | tf_op jit(solution)/shard_map/ppermute | solution.py:320
  7.0 0.8 slice.63
  7.8 1.3 %collective-permute-start.3 = (bf16[2,16,1024]{2,1,0:T(8,128)(2,1)S(1)}, bf16[2,16,1024]{2,1,0:T(8,128)(2,1)S(1)}, u32[]{:S(2)}, u32[]{:S(2)}) collective-permute-start(bf16[2,16,1024]{2,1,0:T(8,128)(2,1)S(1)} %slice.63), channel_id=1, source_target_pairs={{0,4},{4,8},{8,12},{12,16},{16,20},{20,24},{24,28},{1,5},{5,9},{9,... | collective-permute-start | bytes 196616 | tf_op jit(solution)/shard_map/ppermute | solution.py:315
  9.3 0.9 tile.8
  10.1 0.8 copy.16.wstep_ref
  11.0 1.3 %broadcast_in_dim.64.cb_ref = f32[1,2304]{1,0:T(1,128)} reshape(f32[2304]{0:T(1024)} %param.18) | data formatting | bytes 18432 | tf_op jit(solution)/shard_map/broadcast_in_dim | solution.py:383
  12.3 0.7 tile.10
  12.9 0.7 broadcast_in_dim_tile.6.sb_ref
  13.6 0.7 tile.11
  14.2 0.7 broadcast_in_dim_tile.7.dr_ref
  14.9 0.7 broadcast_in_dim.65
  15.6 0.7 broadcast_in_dim_reshape.3.skip_ref
  16.3 1.0 and_convert_fusion.e_ref
  17.3 0.0 collective-permute-done
  17.3 0.0 collective-permute-done.1
  17.4 0.0 collective-permute-done.2
  17.4 0.9 fusion.22
  18.2 0.6 add_subtract_fusion.remaining
  18.9 0.0 collective-permute-done.3.rim_ref
  18.9 0.0 copy-start
  18.9 0.6 copy-done
  19.5 29.5 %scan_terms.1 = (bf16[2,512,2048]{2,1,0:T(8,128)(2,1)}, bf16[2,512,256]{2,1,0:T(8,128)(2,1)}, bf16[2,512,128]{2,1,0:T(8,128)(2,1)}, bf16[2,512,128]{2,1,0:T(8,12...) custom-call(s32[2]{0:T(128)} %add_subtract_fusion.remaining, ...), custom_call_target="tpu_custom_call" | custom-call | flops 4831838208 | bytes 16777216 | tf_op jit(solution)/shard_map/scan_terms/pallas_call | solution.py:335
  48.9 1.3 %slice_bitcast_fusion.1 = (bf16[144,2048]{1,0:T(8,128)(2,1)S(1)}, bf16[144,2048]{1,0:T(8,128)(2,1)S(1)}) fusion(bf16[2,144,2048]{2,1,0:T(8,128)(2,1)} %get-tuple-element.20), kind=kLoop, calls=%fused_computation.15 | loop fusion | bytes 2359296 | tf_op jit(solution)/shard_map/squeeze | solution.py:389
  50.3 2.3 %collective-permute-start.4 = (bf16[144,1024]{1,0:T(8,128)(2,1)S(1)}, bf16[144,1024]{1,0:T(8,128)(2,1)S(1)}, u32[]{:S(2)}, u32[]{:S(2)}) collective-permute-start(bf16[144,1024]{1,0:T(8,128)(2,1)S(1)} %broadcast_select_fusion.6), channel_id=1, source_target_pairs={{0,4},{4,0},{8,12},{12,8},{16,20},{20,16},{24,28},{28,24},{1,5},{5... | collective-permute-start | bytes 884744 | tf_op jit(solution)/shard_map/ppermute | solution.py:258
  52.6 0.1 collective-permute-start.8
  52.7 13.7 %within_blocks.1.part_ref = bf16[2,512,2048]{2,1,0:T(8,128)(2,1)} custom-call(bf16[2,512,2048]{2,1,0:T(8,128)(2,1)} %get-tuple-element.13.x_ref, bf16[2,512,256]{2,1,0:T(8,128)(2,1)} %get-tuple-element.14.bc_ref, bf16[2,512,128]{2,1,0:T(8,128)(2,1)} %get-tuple-element.15.ec_ref, f32[2,512,128]{2,1,0:T(8,128)} %get-tuple-element.16.cum_ref, ...), custom_call_target="tpu_custom_call" | custom-call | flops 8589934592 | bytes 16777216 | tf_op jit(solution)/shard_map/within_blocks/pallas_call | solution.py:394
  66.5 0.0 collective-permute-done.4
  66.5 0.1 broadcast_select_fusion.5
  66.6 0.1 fusion.11
  66.7 0.3 concatenate.22
  67.0 1.6 %collective-permute-start.5 = (bf16[144,1024]{1,0:T(8,128)(2,1)S(1)}, bf16[144,1024]{1,0:T(8,128)(2,1)S(1)}, u32[]{:S(2)}, u32[]{:S(2)}) collective-permute-start(bf16[144,1024]{1,0:T(8,128)(2,1)S(1)} %concatenate.22), channel_id=1, source_target_pairs={{0,8},{4,12},{8,0},{12,4},{16,24},{20,28},{24,16},{28,20},{1,9},{5... | collective-permute-start | bytes 884744 | tf_op jit(solution)/shard_map/ppermute | solution.py:267
  68.6 0.0 collective-permute-done.8
  68.6 0.1 broadcast_select_fusion.1
  68.7 0.1 fusion.10
  68.8 0.3 concatenate.25
  69.1 0.6 collective-permute-start.9
  69.7 7.3 %collective-permute-done.5 = bf16[144,1024]{1,0:T(8,128)(2,1)S(1)} collective-permute-done((bf16[144,1024]{1,0:T(8,128)(2,1)S(1)}, bf16[144,1024]{1,0:T(8,128)(2,1)S(1)}, u32[]{:S(2)}, u32[]{:S(2)}) %collective-permute-start.5) | collective-permute-done | bytes 294944 | tf_op jit(solution)/shard_map/ppermute | solution.py:267
  77.0 0.2 fusion.6
  77.2 0.3 concatenate.23
  77.5 3.4 %collective-permute-start.6 = (bf16[144,1024]{1,0:T(8,128)(2,1)S(1)}, bf16[144,1024]{1,0:T(8,128)(2,1)S(1)}, u32[]{:S(2)}, u32[]{:S(2)}) collective-permute-start(bf16[144,1024]{1,0:T(8,128)(2,1)S(1)} %concatenate.23), channel_id=1, source_target_pairs={{0,16},{4,20},{8,24},{12,28},{1,17},{5,21},{9,25},{13,29},{2,18},{... | collective-permute-start | bytes 884744 | tf_op jit(solution)/shard_map/ppermute | solution.py:267
  80.9 1.7 %collective-permute-done.9 = bf16[144,1024]{1,0:T(8,128)(2,1)S(1)} collective-permute-done((bf16[144,1024]{1,0:T(8,128)(2,1)S(1)}, bf16[144,1024]{1,0:T(8,128)(2,1)S(1)}, u32[]{:S(2)}, u32[]{:S(2)}) %collective-permute-start.9) | collective-permute-done | bytes 294944 | tf_op jit(solution)/shard_map/ppermute | solution.py:267
  82.6 0.2 fusion.9
  82.8 0.3 concatenate.26
  83.1 3.4 %collective-permute-start.10 = (bf16[144,1024]{1,0:T(8,128)(2,1)S(1)}, bf16[144,1024]{1,0:T(8,128)(2,1)S(1)}, u32[]{:S(2)}, u32[]{:S(2)}) collective-permute-start(bf16[144,1024]{1,0:T(8,128)(2,1)S(1)} %concatenate.26), channel_id=1, source_target_pairs={{0,16},{4,20},{8,24},{12,28},{1,17},{5,21},{9,25},{13,29},{2,18},{... | collective-permute-start | bytes 884744 | tf_op jit(solution)/shard_map/ppermute | solution.py:267
  86.6 0.0 collective-permute-done.6
  86.6 0.2 broadcast_select_fusion.15
  86.8 0.1 collective-permute-start.7
  86.9 5.5 %collective-permute-done.10 = bf16[144,1024]{1,0:T(8,128)(2,1)S(1)} collective-permute-done((bf16[144,1024]{1,0:T(8,128)(2,1)S(1)}, bf16[144,1024]{1,0:T(8,128)(2,1)S(1)}, u32[]{:S(2)}, u32[]{:S(2)}) %collective-permute-start.10) | collective-permute-done | bytes 294944 | tf_op jit(solution)/shard_map/ppermute | solution.py:267
  92.4 0.2 broadcast_select_fusion.11
  92.6 0.1 collective-permute-start.11
  92.7 0.0 collective-permute-done.7
  92.8 1.4 %collective-permute-done.11 = bf16[128,1024]{1,0:T(8,128)(2,1)S(1)} collective-permute-done((bf16[128,1024]{1,0:T(8,128)(2,1)S(1)}, bf16[128,1024]{1,0:T(8,128)(2,1)S(1)}, u32[]{:S(2)}, u32[]{:S(2)}) %collective-permute-start.11) | collective-permute-done | bytes 262176 | tf_op jit(solution)/shard_map/ppermute | solution.py:280
  94.3 1.1 pad_maximum_fusion.sin_ref
  95.4 18.5 %gate_and_out.1 = bf16[2,512,1024]{2,1,0:T(8,128)(2,1)} custom-call(s32[2]{0:T(128)} %add_subtract_fusion.remaining, bf16[2,512,1024]{2,1,0:T(8,128)(2,1)} %tok_ref.3, bf16[1024,2048]{1,0:T(8,128)(2,1)} %gp_ref.1, bf16[2,512,2048]{2,1,0:T(8,128)(2,1)} %within_blocks.1.part_ref, bf16[2,512,256]{2,1,0:T(8,128)(2,1)} %get-tuple-element.14.bc_ref, ...), custom_call_target="tpu_custom_call" | custom-call | flops 8589934592 | bytes 20971520 | tf_op jit(solution)/shard_map/gate_and_out/pallas_call | solution.py:416
  (26 shorter events, 0.4 us)
Async XLA Ops:
  0.0 17.3 %collective-permute-start = (s32[2]{0:T(128)}, s32[2]{0:T(128)S(1)}, u32[]{:S(2)}, u32[]{:S(2)}) collective-permute-start(s32[2]{0:T(128)} %param.24), channel_id=1, source_target_pairs={{0,1},{1,2},{2,3},{3,0},{4,5},{5,6},{6,7},{7,4},{8,9},{9,10},{10,1... | collective-permute-start | bytes 32 | tf_op jit(solution)/shard_map/ppermute | solution.py:320
  3.1 14.3 %collective-permute-start.1 = (s32[2]{0:T(128)}, s32[2]{0:T(128)S(1)}, u32[]{:S(2)}, u32[]{:S(2)}) collective-permute-start(s32[2]{0:T(128)} %param.24), channel_id=1, source_target_pairs={{0,2},{1,3},{2,0},{3,1},{4,6},{5,7},{6,4},{7,5},{8,10},{9,11},{10,... | collective-permute-start | bytes 32 | tf_op jit(solution)/shard_map/ppermute | solution.py:320
  5.6 11.7 %collective-permute-start.2 = (s32[2]{0:T(128)}, s32[2]{0:T(128)S(1)}, u32[]{:S(2)}, u32[]{:S(2)}) collective-permute-start(s32[2]{0:T(128)} %param.24), channel_id=1, source_target_pairs={{0,3},{1,0},{2,1},{3,2},{4,7},{5,4},{6,5},{7,6},{8,11},{9,8},{10,9... | collective-permute-start | bytes 32 | tf_op jit(solution)/shard_map/ppermute | solution.py:320
  7.8 11.0 %collective-permute-start.3 = (bf16[2,16,1024]{2,1,0:T(8,128)(2,1)S(1)}, bf16[2,16,1024]{2,1,0:T(8,128)(2,1)S(1)}, u32[]{:S(2)}, u32[]{:S(2)}) collective-permute-start(bf16[2,16,1024]{2,1,0:T(8,128)(2,1)S(1)} %slice.63), channel_id=1, source_target_pairs={{0,4},{4,8},{8,12},{12,16},{16,20},{20,24},{24,28},{1,5},{5,9},{9,... | collective-permute-start | bytes 196616 | tf_op jit(solution)/shard_map/ppermute | solution.py:315
  18.9 0.6 copy-start
  50.3 16.2 %collective-permute-start.4 = (bf16[144,1024]{1,0:T(8,128)(2,1)S(1)}, bf16[144,1024]{1,0:T(8,128)(2,1)S(1)}, u32[]{:S(2)}, u32[]{:S(2)}) collective-permute-start(bf16[144,1024]{1,0:T(8,128)(2,1)S(1)} %broadcast_select_fusion.6), channel_id=1, source_target_pairs={{0,4},{4,0},{8,12},{12,8},{16,20},{20,16},{24,28},{28,24},{1,5},{5... | collective-permute-start | bytes 884744 | tf_op jit(solution)/shard_map/ppermute | solution.py:258
  52.6 15.9 %collective-permute-start.8 = (bf16[144,1024]{1,0:T(8,128)(2,1)S(1)}, bf16[144,1024]{1,0:T(8,128)(2,1)S(1)}, u32[]{:S(2)}, u32[]{:S(2)}) collective-permute-start(bf16[144,1024]{1,0:T(8,128)(2,1)S(1)} %broadcast_select_fusion.2), channel_id=1, source_target_pairs={{0,4},{4,0},{8,12},{12,8},{16,20},{20,16},{24,28},{28,24},{1,5},{5... | collective-permute-start | bytes 884744 | tf_op jit(solution)/shard_map/ppermute | solution.py:258
  67.0 9.9 %collective-permute-start.5 = (bf16[144,1024]{1,0:T(8,128)(2,1)S(1)}, bf16[144,1024]{1,0:T(8,128)(2,1)S(1)}, u32[]{:S(2)}, u32[]{:S(2)}) collective-permute-start(bf16[144,1024]{1,0:T(8,128)(2,1)S(1)} %concatenate.22), channel_id=1, source_target_pairs={{0,8},{4,12},{8,0},{12,4},{16,24},{20,28},{24,16},{28,20},{1,9},{5... | collective-permute-start | bytes 884744 | tf_op jit(solution)/shard_map/ppermute | solution.py:267
  69.1 13.5 %collective-permute-start.9 = (bf16[144,1024]{1,0:T(8,128)(2,1)S(1)}, bf16[144,1024]{1,0:T(8,128)(2,1)S(1)}, u32[]{:S(2)}, u32[]{:S(2)}) collective-permute-start(bf16[144,1024]{1,0:T(8,128)(2,1)S(1)} %concatenate.25), channel_id=1, source_target_pairs={{0,8},{4,12},{8,0},{12,4},{16,24},{20,28},{24,16},{28,20},{1,9},{5... | collective-permute-start | bytes 884744 | tf_op jit(solution)/shard_map/ppermute | solution.py:267
  77.5 9.1 %collective-permute-start.6 = (bf16[144,1024]{1,0:T(8,128)(2,1)S(1)}, bf16[144,1024]{1,0:T(8,128)(2,1)S(1)}, u32[]{:S(2)}, u32[]{:S(2)}) collective-permute-start(bf16[144,1024]{1,0:T(8,128)(2,1)S(1)} %concatenate.23), channel_id=1, source_target_pairs={{0,16},{4,20},{8,24},{12,28},{1,17},{5,21},{9,25},{13,29},{2,18},{... | collective-permute-start | bytes 884744 | tf_op jit(solution)/shard_map/ppermute | solution.py:267
  83.1 9.3 %collective-permute-start.10 = (bf16[144,1024]{1,0:T(8,128)(2,1)S(1)}, bf16[144,1024]{1,0:T(8,128)(2,1)S(1)}, u32[]{:S(2)}, u32[]{:S(2)}) collective-permute-start(bf16[144,1024]{1,0:T(8,128)(2,1)S(1)} %concatenate.26), channel_id=1, source_target_pairs={{0,16},{4,20},{8,24},{12,28},{1,17},{5,21},{9,25},{13,29},{2,18},{... | collective-permute-start | bytes 884744 | tf_op jit(solution)/shard_map/ppermute | solution.py:267
  86.8 5.9 %collective-permute-start.7 = (bf16[128,1024]{1,0:T(8,128)(2,1)S(1)}, bf16[128,1024]{1,0:T(8,128)(2,1)S(1)}, u32[]{:S(2)}, u32[]{:S(2)}) collective-permute-start(bf16[128,1024]{1,0:T(8,128)(2,1)S(1)} %get-tuple-element.25), channel_id=1, source_target_pairs={{0,4},{4,0},{8,12},{12,8},{16,20},{20,16},{24,28},{28,24},{1,5},{5... | collective-permute-start | bytes 786440 | tf_op jit(solution)/shard_map/ppermute | solution.py:280
  92.6 1.6 %collective-permute-start.11 = (bf16[128,1024]{1,0:T(8,128)(2,1)S(1)}, bf16[128,1024]{1,0:T(8,128)(2,1)S(1)}, u32[]{:S(2)}, u32[]{:S(2)}) collective-permute-start(bf16[128,1024]{1,0:T(8,128)(2,1)S(1)} %get-tuple-element.28), channel_id=1, source_target_pairs={{0,4},{4,0},{8,12},{12,8},{16,20},{20,16},{24,28},{28,24},{1,5},{5... | collective-permute-start | bytes 786440 | tf_op jit(solution)/shard_map/ppermute | solution.py:280

commit v2 on v1

v2 whole, which is shorter than its diff:
```python
import functools

import jax
import jax.numpy as jnp
from jax import lax
from jax.experimental import pallas as pl
from jax.experimental.pallas import tpu as pltpu
from jax.sharding import PartitionSpec as P

BLOCK = 256
CHUNK = 256
LANES = 128
TAIL = 16
ROWS = 64
EPSILON = 1e-05
F32 = jnp.float32
BF16 = jnp.bfloat16
VMEM_LIMIT = 60 * 1024 * 1024


def dot(a, b):
    return jnp.dot(a, b, preferred_element_type=F32)


def three_parts(value):
    high = value.astype(BF16)
    rest = value - high.astype(F32)
    mid = rest.astype(BF16)
    low = (rest - mid.astype(F32)).astype(BF16)
    return high, mid, low


def lane_parts(value, heads):
    high, mid, low = three_parts(value)
    group = lax.broadcasted_iota(jnp.int32, value.shape, 1) // heads
    picked = jnp.where(
        group == 0, high.astype(F32), jnp.where(group == 1, mid.astype(F32), low.astype(F32))
    )
    return picked.astype(BF16)


def expand_columns(heads, head_size, start):
    lane = lax.broadcasted_iota(jnp.int32, (LANES, CHUNK), 0)
    column = start + lax.broadcasted_iota(jnp.int32, (LANES, CHUNK), 1)
    same = (lane % heads == column // head_size) & (lane < 3 * heads)
    return jnp.where(same, 1.0, 0.0).astype(BF16)


def head_row(heads, ref):
    lane = lax.broadcasted_iota(jnp.int32, (1, LANES), 1) % heads
    row = jnp.zeros((1, LANES), F32)
    for head in range(heads):
        row = jnp.where(lane == head, ref[head], row)
    return row


def steps_left(held_refs, slot_ref, series, steps):
    groups = len(held_refs)
    place = lax.axis_index("series")
    slot = slot_ref[series]
    total = jnp.int32(0)
    for shift, ref in enumerate(held_refs):
        first = lax.rem(place - shift + groups, groups) * ref.shape[0]
        for index in range(ref.shape[0]):
            total = total + jnp.where(slot == first + index, ref[index], 0)
    return total - lax.axis_index("tm") * steps


def silu(value):
    half = 0.5 * value
    return half + half * jnp.tanh(half)


def scan_kernel(heads, groups, *refs):
    held_refs, refs = refs[:groups], refs[groups:]
    (slot_ref, sb_ref, dr_ref, tok_ref, rim_ref, w_ref, wstep_ref, ck_ref, cb_ref), refs = (
        refs[:9],
        refs[9:],
    )
    x_ref, bc_ref, ec_ref, ed_ref, cum_ref, rt_ref, before_ref, end_ref, raw = refs
    steps = tok_ref.shape[1]
    inner = x_ref.shape[2]
    head_size = inner // heads
    blocks = steps // BLOCK
    taps = ck_ref.shape[0]
    series = pl.program_id(0)
    tokens = tok_ref[0]
    rim = rim_ref[0]

    def convolved(slot, start, put):
        cols = slice(start, start + CHUNK)
        weights = w_ref[:, cols]
        raw[slot, 0:TAIL, :] = dot(rim, weights).astype(BF16).astype(F32)
        raw[slot, TAIL:, :] = dot(tokens, weights).astype(BF16).astype(F32)
        bias = cb_ref[cols][None, :]
        gains = [ck_ref[tap : tap + 1, cols] for tap in range(taps)]
        for row in range(0, steps, ROWS):
            total = bias
            for tap in range(taps):
                first = TAIL - (taps - 1) + tap + row
                total = total + gains[tap] * raw[slot, first : first + ROWS, :]
            put(slice(row, row + ROWS), silu(total).astype(BF16))

    def put_bc(rows, value):
        bc_ref[0, rows, :] = value

    convolved(0, inner, put_bc)
    bc = bc_ref[0]

    wstep = jnp.concatenate([wstep_ref[...]] * (LANES // heads), axis=0)
    step_raw = lax.dot_general(
        tokens, wstep, (((1,), (1,)), ((), ())), preferred_element_type=F32
    ) + head_row(heads, sb_ref)
    soft = jnp.maximum(step_raw, 0.0) + jnp.log1p(jnp.exp(-jnp.abs(step_raw)))
    row = lax.broadcasted_iota(jnp.int32, soft.shape, 0)
    soft = jnp.where(row < steps_left(held_refs, slot_ref, series, steps), soft, 0.0)
    drop = -soft * head_row(heads, dr_ref)
    below = (
        lax.broadcasted_iota(jnp.int32, (BLOCK, BLOCK), 0)
        >= lax.broadcasted_iota(jnp.int32, (BLOCK, BLOCK), 1)
    ).astype(F32).astype(BF16)
    offset = jnp.zeros((1, LANES), F32)
    weight_parts, decay_rows, b_rows = [], [], []
    for block in range(blocks):
        rows = slice(block * BLOCK, (block + 1) * BLOCK)
        high, mid, low = three_parts(drop[rows])
        cum = dot(below, high) + dot(below, mid) + dot(below, low)
        last = cum[BLOCK - 1 : BLOCK]
        cum_ref[0, rows, :] = cum
        ec_ref[0, rows, :] = lane_parts(jnp.exp(cum), heads)
        ed_ref[0, rows, :] = lane_parts(jnp.exp(cum + offset), heads)
        offset = offset + last
        rt_ref[0, block] = (cum - jnp.log(soft[rows])).T[:heads]
        weight_parts.append(lane_parts(jnp.exp(last - cum) * soft[rows], heads))
        decay_rows.append(lane_parts(jnp.exp(last) + jnp.zeros((TAIL, LANES), F32), heads))
        b_rows.append(bc[rows, :LANES].astype(F32).T.astype(BF16))
    device_row = lane_parts(jnp.exp(offset) + jnp.zeros((TAIL, LANES), F32), heads)

    states = bc.shape[1] // 2
    for index, start in enumerate(range(0, inner, CHUNK)):
        cols = slice(start, start + CHUNK)

        def put_x(rows, value, cols=cols):
            x_ref[0, rows, cols] = value

        convolved((index + 1) % 2, start, put_x)
        spread = expand_columns(heads, head_size, start)
        state = None
        for block in range(blocks):
            rows = slice(block * BLOCK, (block + 1) * BLOCK)
            wide = dot(weight_parts[block], spread)
            weighted = (x_ref[0, rows, cols].astype(F32) * wide).astype(BF16)
            added = dot(b_rows[block], weighted)
            if state is None:
                state = added
            else:
                before_ref[0, block - 1, :, cols] = state.astype(BF16)
                state = dot(decay_rows[block], spread)[0:1] * state + added
        end_ref[0, 0:states, cols] = state.astype(BF16)
        decay = dot(device_row, spread)
        high, mid, low = (part.astype(F32) for part in three_parts(decay))
        place = lax.broadcasted_iota(jnp.int32, decay.shape, 0)
        packed = jnp.where(place == 0, high, jnp.where(place == 1, mid, jnp.where(place == 2, low, 0.0)))
        end_ref[0, states:, cols] = packed.astype(BF16)


def within_kernel(heads, skip_ref, x_ref, bc_ref, ec_ref, cum_ref, rt_ref, before_ref, *rest):
    out_ref = rest[-1]
    inner = x_ref.shape[2]
    head_size = inner // heads
    here = pl.program_id(0)
    half = BLOCK // 2
    b_part = bc_ref[0, :, :LANES]
    c_part = bc_ref[0, :, LANES:]
    scores = lax.dot_general(c_part, b_part, (((1,), (1,)), ((), ())), preferred_element_type=F32)
    corner = lax.broadcasted_iota(jnp.int32, (half, half), 0) >= lax.broadcasted_iota(
        jnp.int32, (half, half), 1
    )
    earlier = jnp.where(here > 0, c_part.astype(F32), 0.0).astype(BF16)
    cum = cum_ref[0]
    ec = ec_ref[0]
    empty = jnp.zeros((half, half), BF16)
    lane_head = lax.broadcasted_iota(jnp.int32, (BLOCK, CHUNK), 1) // head_size
    for start in range(0, inner, CHUNK):
        cols = slice(start, start + CHUNK)
        x = x_ref[0, :, cols]
        x_wide = x.astype(F32)
        skip = jnp.zeros((1, CHUNK), F32)
        for local in range(CHUNK // head_size):
            skip = jnp.where(lane_head[:1] == local, skip_ref[start // head_size + local], skip)
        wide = dot(ec, expand_columns(heads, head_size, start))
        base = skip * x_wide + wide * dot(earlier, before_ref[0, 0, :, cols])
        lefts, rights = [], []
        for local in range(CHUNK // head_size):
            head = start // head_size + local
            at = cum[:, head : head + 1]
            of = rt_ref[0, 0, head : head + 1, :]
            first = jnp.where(corner, jnp.exp(jnp.where(corner, at[:half] - of[:, :half], 0.0)), 0.0)
            middle = jnp.exp(at[half:] - of[:, :half])
            last = jnp.where(corner, jnp.exp(jnp.where(corner, at[half:] - of[:, half:], 0.0)), 0.0)
            top = (first * scores[:half, :half]).astype(BF16)
            left = (middle * scores[half:, :half]).astype(BF16)
            right = (last * scores[half:, half:]).astype(BF16)
            lefts.append(
                jnp.concatenate(
                    [
                        jnp.concatenate([top, empty], axis=1),
                        jnp.concatenate([left, right], axis=1),
                    ],
                    axis=0,
                )
            )
            rights.append(jnp.where(lane_head == local, x_wide, 0.0).astype(BF16))
        mixed = dot(jnp.concatenate(lefts, axis=1), jnp.concatenate(rights, axis=0))
        out_ref[0, :, cols] = (mixed + base).astype(out_ref.dtype)


def gate_kernel(tok_ref, gp_ref, out_ref):
    tokens = tok_ref[0]
    for start in range(0, gp_ref.shape[1], CHUNK):
        cols = slice(start, start + CHUNK)
        out_ref[0, :, cols] = silu(dot(tokens, gp_ref[:, cols])).astype(BF16)


def out_kernel(heads, groups, count, *refs):
    held_refs, slot_ref, refs = refs[:groups], refs[groups], refs[groups + 1 :]
    gate_ref, part_ref, bc_ref, ed_ref, gain_ref, op_ref = refs[:6]
    sin_refs, out_ref, gated = refs[6 : 6 + count], refs[-2], refs[-1]
    steps = gate_ref.shape[1]
    inner = gate_ref.shape[2]
    head_size = inner // heads
    series = pl.program_id(0)
    c_part = bc_ref[0, :, LANES:]
    ed = ed_ref[0]
    squares = jnp.zeros((steps, LANES), F32)
    for start in range(0, inner, CHUNK):
        cols = slice(start, start + CHUNK)
        state = sin_refs[0][:, cols]
        for index in range(1, count):
            state = jnp.where(series == index, sin_refs[index][:, cols], state)
        inter = dot(ed, expand_columns(heads, head_size, start)) * dot(c_part, state)
        value = (part_ref[0, :, cols].astype(F32) + inter) * gate_ref[0, :, cols].astype(F32)
        gated[:, cols] = value
        square = value * value
        for lane in range(0, CHUNK, LANES):
            squares = squares + square[:, lane : lane + LANES]
    mean = jnp.sum(squares, axis=1, keepdims=True) / inner
    scale = lax.rsqrt(mean + EPSILON)
    normed = jnp.concatenate(
        [
            (gated[:, start : start + CHUNK] * scale * gain_ref[start : start + CHUNK][None, :]).astype(BF16)
            for start in range(0, inner, CHUNK)
        ],
        axis=1,
    )
    row = lax.broadcasted_iota(jnp.int32, (steps, CHUNK), 0)
    live = row < steps_left(held_refs, slot_ref, series, steps)
    for start in range(0, op_ref.shape[1], CHUNK):
        cols = slice(start, start + CHUNK)
        result = dot(normed, op_ref[:, cols])
        out_ref[0, :, cols] = jnp.where(live, result, 0.0).astype(BF16)


def whole(shape):
    return pl.BlockSpec(shape, lambda *_: (0,) * len(shape))


def per_series(shape):
    return pl.BlockSpec((1,) + shape, lambda s, *_: (s,) + (0,) * len(shape))


def unpack(packed):
    states = packed.shape[0] - TAIL
    tail = packed[states : states + 3].astype(F32)
    return jnp.sum(tail, axis=0, keepdims=True), packed[:states].astype(F32)


def pack(decay, state):
    high = lax.reduce_precision(decay, 8, 7)
    rest = decay - high
    mid = lax.reduce_precision(rest, 8, 7)
    low = rest - mid
    filler = jnp.zeros((TAIL - 3, decay.shape[1]), F32)
    return jnp.concatenate([state, high, mid, low, filler], axis=0).astype(BF16)


def incoming_states(packed, axis, covers):
    count, mine = lax.axis_size(axis), lax.axis_index(axis)
    lanes = range(len(packed))
    half = packed[0].shape[1] // 2
    odd = mine % 2 == 1
    swap = [(i, i ^ 1) for i in range(count)]
    firsts, totals, prefixes = [], [], []
    for one in packed:
        left, right = one[:, :half], one[:, half:]
        got = lax.ppermute(jnp.where(odd, left, right), axis, swap)
        own = jnp.where(odd, right, left)
        first = unpack(jnp.where(odd, got, own))
        second = unpack(jnp.where(odd, own, got))
        firsts.append(first)
        totals.append((first[0] * second[0], second[0] * first[1] + second[1]))
        prefixes.append((jnp.ones_like(first[0]), jnp.zeros_like(first[1])))
    bit = 2
    while bit < count:
        final = bit * 2 >= count
        pairs = [(i, i ^ bit) for i in range(count) if not final or not i & bit]
        later = (mine & bit) != 0
        for lane in lanes:
            total, prefix = totals[lane], prefixes[lane]
            sent = pack(*total)
            if covers and (bit > 2 or lane == lanes[-1]):
                sent = covers.pop(0)(sent)
            other = unpack(lax.ppermute(sent, axis, pairs))
            prefixes[lane] = (
                jnp.where(later, prefix[0] * other[0], prefix[0]),
                jnp.where(later, prefix[0] * other[1] + prefix[1], prefix[1]),
            )
            if not final:
                totals[lane] = (
                    total[0] * other[0],
                    jnp.where(later, total[0] * other[1] + total[1], other[0] * total[1] + other[1]),
                )
        bit *= 2
    outs = []
    for lane in lanes:
        first, prefix = firsts[lane], prefixes[lane][1]
        behind = (first[0] * prefix + first[1]).astype(BF16)
        prefix = prefix.astype(BF16)
        here = jnp.where(odd, behind, prefix)
        there = lax.ppermute(jnp.where(odd, prefix, behind), axis, swap)
        outs.append(
            jnp.concatenate([jnp.where(odd, there, here), jnp.where(odd, here, there)], axis=1)
        )
    return outs


def params():
    return pltpu.CompilerParams(vmem_limit_bytes=VMEM_LIMIT)


def body(
    tokens,
    gate_proj,
    input_proj,
    step_proj,
    conv_kernel,
    conv_bias,
    step_bias,
    decay_rate,
    skip_gain,
    norm_gain,
    out_proj,
    lengths,
    slot_series,
):
    series, steps, model = tokens.shape
    inner = gate_proj.shape[1]
    width = input_proj.shape[1]
    states = (width - inner) // 2
    heads = step_bias.shape[0]
    blocks = steps // BLOCK
    tm, groups = lax.axis_size("tm"), lax.axis_size("series")
    taps = conv_kernel.shape[0]
    rim = lax.ppermute(tokens[:, steps - TAIL :], "tm", [(i, i + 1) for i in range(tm - 1)])
    held = [lengths]
    for shift in range(1, groups):
        held.append(lax.ppermute(lengths, "series", [(i, (i + shift) % groups) for i in range(groups)]))

    smem = pl.BlockSpec(memory_space=pltpu.SMEM)
    x, bc, ec, ed, cum, rt, before, end = pl.pallas_call(
        functools.partial(scan_kernel, heads, groups),
        grid=(series,),
        in_specs=[
            *[smem] * (groups + 3),
            per_series((steps, model)),
            per_series((TAIL, model)),
            whole((model, width)),
            whole((heads, model)),
            whole((taps, width)),
            whole((width,)),
        ],
        out_specs=[
            per_series((steps, inner)),
            per_series((steps, width - inner)),
            per_series((steps, LANES)),
            per_series((steps, LANES)),
            per_series((steps, LANES)),
            per_series((blocks, heads, BLOCK)),
            per_series((max(blocks - 1, 1), states, inner)),
            per_series((states + TAIL, inner)),
        ],
        out_shape=[
            jax.ShapeDtypeStruct((series, steps, inner), BF16),
            jax.ShapeDtypeStruct((series, steps, width - inner), BF16),
            jax.ShapeDtypeStruct((series, steps, LANES), BF16),
            jax.ShapeDtypeStruct((series, steps, LANES), BF16),
            jax.ShapeDtypeStruct((series, steps, LANES), F32),
            jax.ShapeDtypeStruct((series, blocks, heads, BLOCK), F32),
            jax.ShapeDtypeStruct((series, max(blocks - 1, 1), states, inner), BF16),
            jax.ShapeDtypeStruct((series, states + TAIL, inner), BF16),
        ],
        scratch_shapes=[pltpu.VMEM((2, steps + TAIL, CHUNK), F32)],
        compiler_params=params(),
        cost_estimate=pl.CostEstimate(
            flops=2 * series * steps * model * width, bytes_accessed=16 << 20, transcendentals=0
        ),
        name="scan_terms",
    )(
        *held,
        slot_series,
        step_bias,
        decay_rate,
        tokens,
        rim,
        input_proj,
        step_proj.T,
        conv_kernel,
        conv_bias,
    )

    def within(one, cum, partial):
        def per_block(shape):
            return pl.BlockSpec((1, BLOCK) + shape, lambda b: (one, b) + (0,) * len(shape))

        earlier = [] if partial is None else [partial]
        return pl.pallas_call(
            functools.partial(within_kernel, heads),
            grid=(blocks,),
            in_specs=[
                smem,
                per_block((inner,)),
                per_block((width - inner,)),
                per_block((LANES,)),
                per_block((LANES,)),
                pl.BlockSpec((1, 1, heads, BLOCK), lambda b: (one, b, 0, 0)),
                pl.BlockSpec((1, 1, states, inner), lambda b: (one, jnp.maximum(b - 1, 0), 0, 0)),
            ]
            + [pl.BlockSpec(memory_space=pl.ANY)] * len(earlier),
            out_specs=per_block((inner,)),
            out_shape=jax.ShapeDtypeStruct((series, steps, inner), BF16),
            input_output_aliases={7: 0} if earlier else {},
            compiler_params=params(),
            cost_estimate=pl.CostEstimate(
                flops=16 * steps * BLOCK * inner, bytes_accessed=8 << 20, transcendentals=0
            ),
            name="within_blocks",
        )(skip_gain, x, bc, ec, cum, rt, before, *earlier)

    done = {"cum": cum, "partial": None}

    def cover_within(one):
        def run(sent):
            sent, ready = lax.optimization_barrier((sent, done["cum"]))
            done["partial"] = within(one, ready, done["partial"])
            return sent

        return run

    def gates(tokens):
        return pl.pallas_call(
            gate_kernel,
            grid=(series,),
            in_specs=[per_series((steps, model)), whole((model, inner))],
            out_specs=per_series((steps, inner)),
            out_shape=jax.ShapeDtypeStruct((series, steps, inner), BF16),
            compiler_params=params(),
            cost_estimate=pl.CostEstimate(
                flops=2 * series * steps * model * inner, bytes_accessed=10 << 20, transcendentals=0
            ),
            name="gates",
        )(tokens, gate_proj)

    def cover_gates(sent):
        sent, ready = lax.optimization_barrier((sent, tokens))
        done["gate"] = gates(ready)
        return sent

    covers = [cover_within(one) for one in range(series)] + [cover_gates]
    incoming = incoming_states([end[s] for s in range(series)], "tm", covers)
    for cover in covers:
        cover(incoming[-1])

    return pl.pallas_call(
        functools.partial(out_kernel, heads, groups, series),
        grid=(series,),
        in_specs=[
            *[smem] * (groups + 1),
            per_series((steps, inner)),
            per_series((steps, inner)),
            per_series((steps, width - inner)),
            per_series((steps, LANES)),
            whole((inner,)),
            whole((inner, model)),
        ]
        + [whole((states, inner))] * series,
        out_specs=per_series((steps, model)),
        out_shape=jax.ShapeDtypeStruct((series, steps, model), BF16),
        scratch_shapes=[pltpu.VMEM((steps, inner), F32)],
        compiler_params=params(),
        cost_estimate=pl.CostEstimate(
            flops=2 * series * steps * model * inner, bytes_accessed=16 << 20, transcendentals=0
        ),
        name="gate_and_out",
    )(*held, slot_series, done["gate"], done["partial"], bc, ed, norm_gain, out_proj, *incoming)


def solution(mesh):
    in_specs = (P("series", "tm", None),) + (P(),) * 10 + (P("series"), P("series"))
    return jax.shard_map(
        body, mesh=mesh, in_specs=in_specs, out_specs=P("series", "tm", None), check_vma=False
    )
```

time: 114 us -> 98.5 us (0.86)
  waiting for transfers between devices: 15.8 us -> 4.76 us
  local copies, waits for them, and re-layouts: 10.9 us -> 3.89 us
  Pallas kernels: 61.7 us -> 66.8 us
  other arithmetic: 5.15 us -> 3.15 us
    ppermute x8, waiting for transfers between devices: 15.8 us -> 2.41 us  [the longest x2 0.97 us: incoming_states(): got = lax.ppermute(jnp.where(odd, left, right), axis, swap)]
    pallas_call x3 -> x5, Pallas kernels: 61.7 us -> 66.8 us  [the longest x1 29.1 us: body(): pl.pallas_call(functools.partial(scan_kernel, heads, groups), grid=(serie...]
    another operation x8 -> x1, local copies, waits for them, and re-layouts: 5 us -> 0.01 us  [the longest x2 1.69 us: body(): step_wide = jnp.tile(step_proj, (1, copies))]
    ppermute x3, waiting for transfers between devices: 0.01 us -> 2.35 us  [body(): lax.ppermute(lengths, 'series', [(i, (i + shift) % groups) for i in range...]
    broadcast_in_dim x2 -> x0, local copies, waits for them, and re-layouts: 2.03 us -> none  [the longest x1 1.3 us: body(): conv_bias[None]]
    concatenate x0 -> x2, other arithmetic: none -> 1.72 us  [incoming_states(): jnp.concatenate([jnp.where(odd, there, here), jnp.where(odd, here, there)...]
    another operation x11 -> x8, other arithmetic: 1.77 us -> 0.62 us  [the longest x3 1.16 us: body(): incoming = jnp.stack([incoming_state(end[s], 'tm') for s in range(series)])]
  transfers between devices with their start and end apart: 12 -> 12, of which waited for: 4 -> 5; matrix products, arithmetic and copies ran while one was open for 11% -> 3% of each run, Pallas kernels for 12% -> 25%
where the time goes in v2:
time: 98.5 us; the launch traced here: 98.3 us
  Pallas kernels  66.8 us (68%)
  starting transfers between devices  19.4 us (20%)
  waiting for transfers between devices  4.76 us (5%)
  local copies, waits for them, and re-layouts  3.89 us (4%)
  other arithmetic  3.15 us (3%)
    pallas_call x1, Pallas kernels, body(): pl.pallas_call(functools.partial(scan_kernel, heads, groups), grid=(serie...  29.1 us
    pallas_call x2, Pallas kernels, within(): pl.pallas_call(functools.partial(within_kernel, heads), grid=(blocks,), i...  15.9 us
    pallas_call x1, Pallas kernels, body(): pl.pallas_call(functools.partial(out_kernel, heads, groups, series), grid...  12.8 us
    ppermute x4, starting transfers between devices, incoming_states(): other = unpack(lax.ppermute(sent, axis, pairs))  9.39 us
    pallas_call x1, Pallas kernels, gates(): pl.pallas_call(gate_kernel, grid=(series,), in_specs=[per_series((steps,...  9.04 us
    ppermute x3, starting transfers between devices, body(): lax.ppermute(lengths, 'series', [(i, (i + shift) % groups) for i in range...  6.38 us
    ppermute x1, starting transfers between devices, body(): lax.ppermute(tokens[:, steps - TAIL:], 'tm', [(i, i + 1) for i in range(t...  2.39 us
    ppermute x3, waiting for transfers between devices, body(): lax.ppermute(lengths, 'series', [(i, (i + shift) % groups) for i in range...  2.35 us
  transfers between devices with their start and end apart: 12, of which 5 were waited for; matrix products, arithmetic and copies ran while one was open for 3% of the time, Pallas kernels for 25%

profile of v2, /device:TPU:0, one launch (start us, length us, event | category | flops | bytes accessed | tf_op | source)
XLA Modules:
  0.0 98.3 jit_solution(9490128775146876622)
XLA Ops:
  0.0 0.8 slice.63
  0.8 2.4 %collective-permute-start.3 = (bf16[2,16,1024]{2,1,0:T(8,128)(2,1)S(1)}, bf16[2,16,1024]{2,1,0:T(8,128)(2,1)S(1)}, u32[]{:S(2)}, u32[]{:S(2)}) collective-permute-start(bf16[2,16,1024]{2,1,0:T(8,128)(2,1)S(1)} %slice.63), channel_id=1, source_target_pairs={{0,4},{4,8},{8,12},{12,16},{16,20},{20,24},{24,28},{1,5},{5,9},{9,... | collective-permute-start | bytes 196616 | tf_op jit(solution)/shard_map/ppermute | solution.py:364
  3.2 2.4 %collective-permute-start = (s32[2]{0:T(128)}, s32[2]{0:T(128)S(1)}, u32[]{:S(2)}, u32[]{:S(2)}) collective-permute-start(s32[2]{0:T(128)} %refs_0_.3), channel_id=1, source_target_pairs={{0,1},{1,2},{2,3},{3,0},{4,5},{5,6},{6,7},{7,4},{8,9},{9,10},{10,1... | collective-permute-start | bytes 32 | tf_op jit(solution)/shard_map/ppermute | solution.py:367
  5.7 2.6 %collective-permute-start.1 = (s32[2]{0:T(128)}, s32[2]{0:T(128)S(1)}, u32[]{:S(2)}, u32[]{:S(2)}) collective-permute-start(s32[2]{0:T(128)} %refs_0_.3), channel_id=1, source_target_pairs={{0,2},{1,3},{2,0},{3,1},{4,6},{5,7},{6,4},{7,5},{8,10},{9,11},{10,... | collective-permute-start | bytes 32 | tf_op jit(solution)/shard_map/ppermute | solution.py:367
  8.3 1.3 %collective-permute-start.2 = (s32[2]{0:T(128)}, s32[2]{0:T(128)S(1)}, u32[]{:S(2)}, u32[]{:S(2)}) collective-permute-start(s32[2]{0:T(128)} %refs_0_.3), channel_id=1, source_target_pairs={{0,3},{1,0},{2,1},{3,2},{4,7},{5,4},{6,5},{7,6},{8,11},{9,8},{10,9... | collective-permute-start | bytes 32 | tf_op jit(solution)/shard_map/ppermute | solution.py:367
  9.6 0.0 collective-permute-done.refs_1_
  9.6 0.0 copy-start
  9.6 0.7 collective-permute-done.1.refs_2_
  10.3 0.0 copy-start.1
  10.3 1.7 %collective-permute-done.2.refs_3_ = s32[2]{0:T(128)S(1)} collective-permute-done((s32[2]{0:T(128)}, s32[2]{0:T(128)S(1)}, u32[]{:S(2)}, u32[]{:S(2)}) %collective-permute-start.2) | collective-permute-done | bytes 40 | tf_op jit(solution)/shard_map/ppermute | solution.py:367
  12.0 0.0 copy-start.2
  12.0 0.0 collective-permute-done.3.refs_8_
  12.0 0.0 copy-start.3
  12.0 0.0 copy-done
  12.0 0.0 copy-done.1
  12.0 0.5 copy-done.2
  12.6 0.1 copy-done.3
  12.6 29.1 %scan_terms.1 = (bf16[2,512,2048]{2,1,0:T(8,128)(2,1)}, bf16[2,512,256]{2,1,0:T(8,128)(2,1)}, bf16[2,512,128]{2,1,0:T(8,128)(2,1)}, bf16[2,512,128]{2,1,0:T(8,12...) custom-call(s32[2]{0:T(128)} %refs_0_.3, ...), custom_call_target="tpu_custom_call" | custom-call | flops 4831838208 | bytes 16777216 | tf_op jit(solution)/shard_map/scan_terms/pallas_call | solution.py:370
  41.7 1.3 %slice_bitcast_fusion = (bf16[144,2048]{1,0:T(8,128)(2,1)S(1)}, bf16[144,2048]{1,0:T(8,128)(2,1)S(1)}) fusion(bf16[2,144,2048]{2,1,0:T(8,128)(2,1)} %get-tuple-element.19), kind=kLoop, calls=%fused_computation.12 | loop fusion | bytes 2359296 | tf_op jit(solution)/shard_map/squeeze | solution.py:479
  43.1 0.1 collective-permute-start.4
  43.2 0.5 collective-permute-start.6
  43.7 1.0 collective-permute-done.4
  44.7 0.1 broadcast_select_fusion.5
  44.8 0.1 fusion.11
  44.9 0.3 concatenate.22
  45.2 1.7 %collective-permute-start.5 = (bf16[144,1024]{1,0:T(8,128)(2,1)S(1)}, bf16[144,1024]{1,0:T(8,128)(2,1)S(1)}, u32[]{:S(2)}, u32[]{:S(2)}) collective-permute-start(bf16[144,1024]{1,0:T(8,128)(2,1)S(1)} %concatenate.22), channel_id=1, source_target_pairs={{0,8},{4,12},{8,0},{12,4},{16,24},{20,28},{24,16},{28,20},{1,9},{5... | collective-permute-start | bytes 884744 | tf_op jit(solution)/shard_map/ppermute | solution.py:313
  47.0 0.0 collective-permute-done.6
  47.0 0.1 broadcast_select_fusion.1
  47.1 0.1 fusion.10
  47.2 0.3 concatenate.24
  47.5 0.4 collective-permute-start.7
  47.9 7.9 %within_blocks.2.rest_0_ = bf16[2,512,2048]{2,1,0:T(8,128)(2,1)} custom-call(f32[32]{0:T(128)} %skip_ref.3, bf16[2,512,2048]{2,1,0:T(8,128)(2,1)} %get-tuple-element.23.x_ref, bf16[2,512,256]{2,1,0:T(8,128)(2,1)} %get-tuple-element.24.bc_ref.refs_7_, bf16[2,512,128]{2,1,0:T(8,128)(2,1)} %get-tuple-element.25.ec_ref, ...), custom_call_target="tpu_custom_call" | custom-call | flops 4294967296 | bytes 8388608 | tf_op jit(solution)/shard_map/within_blocks/pallas_call | solution.py:426
  55.8 0.0 collective-permute-done.5
  55.9 0.2 fusion.6
  56.1 0.3 concatenate.23
  56.3 3.6 %collective-permute-start.10 = (bf16[144,1024]{1,0:T(8,128)(2,1)S(1)}, bf16[144,1024]{1,0:T(8,128)(2,1)S(1)}, u32[]{:S(2)}, u32[]{:S(2)}) collective-permute-start(bf16[144,1024]{1,0:T(8,128)(2,1)S(1)} %concatenate.23), channel_id=1, source_target_pairs={{0,16},{4,20},{8,24},{12,28},{1,17},{5,21},{9,25},{13,29},{2,18},{... | collective-permute-start | bytes 884744 | tf_op jit(solution)/shard_map/ppermute | solution.py:313
  60.0 0.7 collective-permute-done.7
  60.7 0.2 fusion.9
  60.9 0.3 concatenate.25
  61.2 3.6 %collective-permute-start.8 = (bf16[144,1024]{1,0:T(8,128)(2,1)S(1)}, bf16[144,1024]{1,0:T(8,128)(2,1)S(1)}, u32[]{:S(2)}, u32[]{:S(2)}) collective-permute-start(bf16[144,1024]{1,0:T(8,128)(2,1)S(1)} %concatenate.25), channel_id=1, source_target_pairs={{0,16},{4,20},{8,24},{12,28},{1,17},{5,21},{9,25},{13,29},{2,18},{... | collective-permute-start | bytes 884744 | tf_op jit(solution)/shard_map/ppermute | solution.py:313
  64.8 8.0 %within_blocks.3.refs_6_ = bf16[2,512,2048]{2,1,0:T(8,128)(2,1)} custom-call(f32[32]{0:T(128)} %skip_ref.3, bf16[2,512,2048]{2,1,0:T(8,128)(2,1)} %get-tuple-element.23.x_ref, bf16[2,512,256]{2,1,0:T(8,128)(2,1)} %get-tuple-element.24.bc_ref.refs_7_, bf16[2,512,128]{2,1,0:T(8,128)(2,1)} %get-tuple-element.25.ec_ref, ...), custom_call_target="tpu_custom_call", output_to_operand_aliasing={{}: (7, {})} | custom-call | flops 4294967296 | bytes 8388608 | tf_op jit(solution)/shard_map/within_blocks/pallas_call | solution.py:426
  72.8 9.0 %gates.1.refs_5_ = bf16[2,512,2048]{2,1,0:T(8,128)(2,1)} custom-call(bf16[2,512,1024]{2,1,0:T(8,128)(2,1)} %tok_ref, bf16[1024,2048]{1,0:T(8,128)(2,1)} %gp_ref.1), custom_call_target="tpu_custom_call" | custom-call | flops 4294967296 | bytes 10485760 | tf_op jit(solution)/shard_map/gates/pallas_call | solution.py:460
  81.8 0.0 collective-permute-done.10
  81.8 0.2 broadcast_select_fusion.11
  82.1 0.1 collective-permute-start.11
  82.1 0.0 collective-permute-done.8
  82.2 0.2 broadcast_select_fusion.15
  82.4 0.6 collective-permute-start.9
  82.9 0.7 collective-permute-done.11
  83.7 0.9 pad_maximum_fusion.1.refs_12_
  84.6 0.0 collective-permute-done.9
  84.6 0.9 pad_maximum_fusion.refs_11_
  85.5 12.8 %gate_and_out.1 = bf16[2,512,1024]{2,1,0:T(8,128)(2,1)} custom-call(s32[2]{0:T(128)} %refs_0_.3, s32[2]{0:T(128)} %copy-done, s32[2]{0:T(128)} %copy-done.1, s32[2]{0:T(128)} %copy-done.2, s32[2]{0:T(128)} %refs_4_.3, bf16[2,512,2048]{2,1,0:T(8,128)(2,1)} %gates.1.refs_5_, bf16[2,512,2048]{2,1,0:T(8,128)(2,1)} %within_blocks.3.refs_6_, ...), custom_call_target="tpu_custom_call" | custom-call | flops 4294967296 | bytes 16777216 | tf_op jit(solution)/shard_map/gate_and_out/pallas_call | solution.py:483
  (17 shorter events, 0.3 us)
Async XLA Ops:
  0.8 11.1 %collective-permute-start.3 = (bf16[2,16,1024]{2,1,0:T(8,128)(2,1)S(1)}, bf16[2,16,1024]{2,1,0:T(8,128)(2,1)S(1)}, u32[]{:S(2)}, u32[]{:S(2)}) collective-permute-start(bf16[2,16,1024]{2,1,0:T(8,128)(2,1)S(1)} %slice.63), channel_id=1, source_target_pairs={{0,4},{4,8},{8,12},{12,16},{16,20},{20,24},{24,28},{1,5},{5,9},{9,... | collective-permute-start | bytes 196616 | tf_op jit(solution)/shard_map/ppermute | solution.py:364
  3.2 6.4 %collective-permute-start = (s32[2]{0:T(128)}, s32[2]{0:T(128)S(1)}, u32[]{:S(2)}, u32[]{:S(2)}) collective-permute-start(s32[2]{0:T(128)} %refs_0_.3), channel_id=1, source_target_pairs={{0,1},{1,2},{2,3},{3,0},{4,5},{5,6},{6,7},{7,4},{8,9},{9,10},{10,1... | collective-permute-start | bytes 32 | tf_op jit(solution)/shard_map/ppermute | solution.py:367
  5.7 4.6 %collective-permute-start.1 = (s32[2]{0:T(128)}, s32[2]{0:T(128)S(1)}, u32[]{:S(2)}, u32[]{:S(2)}) collective-permute-start(s32[2]{0:T(128)} %refs_0_.3), channel_id=1, source_target_pairs={{0,2},{1,3},{2,0},{3,1},{4,6},{5,7},{6,4},{7,5},{8,10},{9,11},{10,... | collective-permute-start | bytes 32 | tf_op jit(solution)/shard_map/ppermute | solution.py:367
  8.3 3.7 %collective-permute-start.2 = (s32[2]{0:T(128)}, s32[2]{0:T(128)S(1)}, u32[]{:S(2)}, u32[]{:S(2)}) collective-permute-start(s32[2]{0:T(128)} %refs_0_.3), channel_id=1, source_target_pairs={{0,3},{1,0},{2,1},{3,2},{4,7},{5,4},{6,5},{7,6},{8,11},{9,8},{10,9... | collective-permute-start | bytes 32 | tf_op jit(solution)/shard_map/ppermute | solution.py:367
  9.6 2.4 %copy-start = (s32[2]{0:T(128)}, s32[2]{0:T(128)S(1)}, u32[]{:S(2)}) copy-start(s32[2]{0:T(128)S(1)} %collective-permute-done.refs_1_) | copy-start | bytes 28
  10.3 1.7 %copy-start.1 = (s32[2]{0:T(128)}, s32[2]{0:T(128)S(1)}, u32[]{:S(2)}) copy-start(s32[2]{0:T(128)S(1)} %collective-permute-done.1.refs_2_) | copy-start | bytes 28
  12.0 0.6 copy-start.2
  12.0 0.6 copy-start.3
  43.1 1.6 %collective-permute-start.4 = (bf16[144,1024]{1,0:T(8,128)(2,1)S(1)}, bf16[144,1024]{1,0:T(8,128)(2,1)S(1)}, u32[]{:S(2)}, u32[]{:S(2)}) collective-permute-start(bf16[144,1024]{1,0:T(8,128)(2,1)S(1)} %broadcast_select_fusion.7), channel_id=1, source_target_pairs={{0,4},{4,0},{8,12},{12,8},{16,20},{20,16},{24,28},{28,24},{1,5},{5... | collective-permute-start | bytes 884744 | tf_op jit(solution)/shard_map/ppermute | solution.py:296
  43.2 3.7 %collective-permute-start.6 = (bf16[144,1024]{1,0:T(8,128)(2,1)S(1)}, bf16[144,1024]{1,0:T(8,128)(2,1)S(1)}, u32[]{:S(2)}, u32[]{:S(2)}) collective-permute-start(bf16[144,1024]{1,0:T(8,128)(2,1)S(1)} %broadcast_select_fusion.3), channel_id=1, source_target_pairs={{0,4},{4,0},{8,12},{12,8},{16,20},{20,16},{24,28},{28,24},{1,5},{5... | collective-permute-start | bytes 884744 | tf_op jit(solution)/shard_map/ppermute | solution.py:296
  45.2 10.6 %collective-permute-start.5 = (bf16[144,1024]{1,0:T(8,128)(2,1)S(1)}, bf16[144,1024]{1,0:T(8,128)(2,1)S(1)}, u32[]{:S(2)}, u32[]{:S(2)}) collective-permute-start(bf16[144,1024]{1,0:T(8,128)(2,1)S(1)} %concatenate.22), channel_id=1, source_target_pairs={{0,8},{4,12},{8,0},{12,4},{16,24},{20,28},{24,16},{28,20},{1,9},{5... | collective-permute-start | bytes 884744 | tf_op jit(solution)/shard_map/ppermute | solution.py:313
  47.5 13.2 %collective-permute-start.7 = (bf16[144,1024]{1,0:T(8,128)(2,1)S(1)}, bf16[144,1024]{1,0:T(8,128)(2,1)S(1)}, u32[]{:S(2)}, u32[]{:S(2)}) collective-permute-start(bf16[144,1024]{1,0:T(8,128)(2,1)S(1)} %concatenate.24), channel_id=1, source_target_pairs={{0,8},{4,12},{8,0},{12,4},{16,24},{20,28},{24,16},{28,20},{1,9},{5... | collective-permute-start | bytes 884744 | tf_op jit(solution)/shard_map/ppermute | solution.py:313
  56.3 25.5 %collective-permute-start.10 = (bf16[144,1024]{1,0:T(8,128)(2,1)S(1)}, bf16[144,1024]{1,0:T(8,128)(2,1)S(1)}, u32[]{:S(2)}, u32[]{:S(2)}) collective-permute-start(bf16[144,1024]{1,0:T(8,128)(2,1)S(1)} %concatenate.23), channel_id=1, source_target_pairs={{0,16},{4,20},{8,24},{12,28},{1,17},{5,21},{9,25},{13,29},{2,18},{... | collective-permute-start | bytes 884744 | tf_op jit(solution)/shard_map/ppermute | solution.py:313
  61.2 21.0 %collective-permute-start.8 = (bf16[144,1024]{1,0:T(8,128)(2,1)S(1)}, bf16[144,1024]{1,0:T(8,128)(2,1)S(1)}, u32[]{:S(2)}, u32[]{:S(2)}) collective-permute-start(bf16[144,1024]{1,0:T(8,128)(2,1)S(1)} %concatenate.25), channel_id=1, source_target_pairs={{0,16},{4,20},{8,24},{12,28},{1,17},{5,21},{9,25},{13,29},{2,18},{... | collective-permute-start | bytes 884744 | tf_op jit(solution)/shard_map/ppermute | solution.py:313
  82.1 1.6 %collective-permute-start.11 = (bf16[128,1024]{1,0:T(8,128)(2,1)S(1)}, bf16[128,1024]{1,0:T(8,128)(2,1)S(1)}, u32[]{:S(2)}, u32[]{:S(2)}) collective-permute-start(bf16[128,1024]{1,0:T(8,128)(2,1)S(1)} %get-tuple-element.33), channel_id=1, source_target_pairs={{0,4},{4,0},{8,12},{12,8},{16,20},{20,16},{24,28},{28,24},{1,5},{5... | collective-permute-start | bytes 786440 | tf_op jit(solution)/shard_map/ppermute | solution.py:330
  82.4 2.2 %collective-permute-start.9 = (bf16[128,1024]{1,0:T(8,128)(2,1)S(1)}, bf16[128,1024]{1,0:T(8,128)(2,1)S(1)}, u32[]{:S(2)}, u32[]{:S(2)}) collective-permute-start(bf16[128,1024]{1,0:T(8,128)(2,1)S(1)} %get-tuple-element.36), channel_id=1, source_target_pairs={{0,4},{4,0},{8,12},{12,8},{16,20},{20,16},{24,28},{28,24},{1,5},{5... | collective-permute-start | bytes 786440 | tf_op jit(solution)/shard_map/ppermute | solution.py:330
